TPU v7x, 256 devices: a whole 4x4x8 slice. The times are simulated.
256 devices in a mesh: gx: 64 (over x, z, core), col: 4 (over y).
Axes of the slice: x: 4, y: 4, z: 8, core: 2. Of those that a mesh axis runs over, the one named last changes fastest.
Arguments:
- grid_field: bfloat16 [64, 256, 256, 128], P('col', 'gx'), may hold values from -6 to 6
- tucker_core: float32 [2, 32, 32, 8, 8, 4], P(None, 'col'), may hold values from -1.5 to 1.5
- in_factor: float32 [64, 32], P('col'), may hold values from -0.75 to 0.75
- out_factor: float32 [64, 32], P('col'), may hold values from -1 to 1
- x_factor: float32 [32, 8], replicated, may hold values from -4 to 4
- y_factor: float32 [32, 8], replicated, may hold values from -4 to 4
- z_factor: float32 [16, 4], replicated, may hold values from -4 to 4
- kx_reach: int32 [32, 16], replicated, may hold values from 1 to 17
Outputs:
- spectral_out: bfloat16 [64, 256, 256, 128], P('col', 'gx')
All inputs are finite; a program needn't handle non-finite values.
Results may differ from a plain program's by a relative error of at most 0.001.
Values sent between devices are 32-bit elements; how exact they have to be, the bound alone decides.
No kernel may reach another device: no remote copies, remote signals or barrier semaphores. Data moves between devices by JAX's collectives and lax.ppermute only.
A program may use at most 64 MiB of HBM per device.

v0:
```python
import math

import jax
import jax.numpy as jnp
from jax import lax
from jax.sharding import PartitionSpec as P


def split_up(shard, dim, devices):
    dims = shard.shape
    pieces = shard.reshape(*dims[:dim], devices, dims[dim] // devices, *dims[dim + 1 :])
    return jnp.moveaxis(pieces, dim, 0)


def summed_on_arrival(shard, axis, dim):
    pieces = split_up(shard, dim, lax.axis_size(axis))
    arrived = lax.all_to_all(pieces, axis, split_axis=0, concat_axis=0, tiled=True)
    return arrived.sum(axis=0)


def copy_for_each(shard, axis):
    devices = lax.axis_size(axis)
    return lax.all_to_all(
        jnp.broadcast_to(shard[None], (devices, *shard.shape)), axis, 0, 0, tiled=True
    )


def taken_together(shard, axis):
    return copy_for_each(shard, axis).sum(axis=0)


def slot_freq(slot_count):
    slot_index = jnp.arange(slot_count, dtype=jnp.int32)
    return jnp.where(slot_index < slot_count // 2, slot_index, slot_index - slot_count)


def phase_table(positions, extent, slot_count, direction):
    phase_steps = positions[:, None] * slot_freq(slot_count)[None, :] % extent
    radians = 2.0 * math.pi / extent * phase_steps.astype(jnp.float32)
    norm_scale = 1.0 / math.sqrt(extent)
    cosine = jnp.cos(radians) * norm_scale
    sine_part = direction * jnp.sin(radians) * norm_scale
    return jnp.stack([jnp.stack([cosine, -sine_part], 1), jnp.stack([sine_part, cosine], 1)], 1)


def z_tables(grid_z, modes_z):
    z_index = jnp.arange(grid_z, dtype=jnp.int32)
    kz_index = jnp.arange(modes_z, dtype=jnp.int32)
    phase_steps = z_index[:, None] * kz_index[None, :] % grid_z
    radians = 2.0 * math.pi / grid_z * phase_steps.astype(jnp.float32)
    norm_scale = 1.0 / math.sqrt(grid_z)
    cosine = jnp.cos(radians) * norm_scale
    sine_part = jnp.sin(radians) * norm_scale
    forward = jnp.stack([cosine, -sine_part], 1)
    weight = jnp.where(kz_index == 0, 1.0, 2.0).astype(jnp.float32)
    backward = jnp.stack([(cosine * weight[None, :]).T, -(sine_part * weight[None, :]).T], 0)
    return (forward, backward)


def per_device(
    grid_field, tucker_core, in_factor, out_factor, x_factor, y_factor, z_factor, kx_reach
):
    highest = lax.Precision.HIGHEST
    channels, planes, grid_y, grid_z = grid_field.shape
    modes_x = x_factor.shape[0]
    modes_y = y_factor.shape[0]
    modes_z = z_factor.shape[0]
    width_gx = lax.axis_size("gx")
    grid_x = planes * width_gx
    columns = modes_y * modes_z
    col_dev = columns // width_gx
    slab_index = lax.axis_index("gx")
    z_forward, z_backward = z_tables(grid_z, modes_z)
    y_forward = phase_table(jnp.arange(grid_y, dtype=jnp.int32), grid_y, modes_y, 1.0)
    x_forward = phase_table(jnp.arange(grid_x, dtype=jnp.int32), grid_x, modes_x, 1.0)
    values = grid_field.astype(jnp.float32)
    z_spectrum = jnp.einsum("cxyz,zpl->cxply", values, z_forward, precision=highest)
    y_spectrum = jnp.einsum("cxply,ypqj->qcxjl", z_spectrum, y_forward, precision=highest)
    y_spectrum = y_spectrum.reshape(2, channels, planes, columns)
    first_col = slab_index * col_dev
    reach_dev = lax.dynamic_slice_in_dim(kx_reach.reshape(-1), first_col, col_dev)
    kept_mask = (jnp.abs(slot_freq(modes_x))[:, None] < reach_dev[None, :]).astype(jnp.float32)
    arrived = lax.all_to_all(y_spectrum, "gx", split_axis=3, concat_axis=2, tiled=True)
    spectrum = jnp.einsum("pcxm,xpqk->qckm", arrived, x_forward, precision=highest)
    partial_value = jnp.einsum("qckm,cr->qrkm", spectrum, in_factor, precision=highest)
    amplitude = summed_on_arrival(partial_value, "col", 1)
    amplitude = amplitude * kept_mask[None, None]
    column = first_col + jnp.arange(col_dev, dtype=jnp.int32)
    pick_y = (column[:, None] // modes_z == jnp.arange(modes_y, dtype=jnp.int32)[None, :]).astype(
        jnp.float32
    )
    pick_z = (column[:, None] % modes_z == jnp.arange(modes_z, dtype=jnp.int32)[None, :]).astype(
        jnp.float32
    )
    y_rows = jnp.dot(pick_y, y_factor, precision=highest)
    z_rows = jnp.dot(pick_z, z_factor, precision=highest)
    core_cols = jnp.einsum("prsabe,mb,me->prsam", tucker_core, y_rows, z_rows, precision=highest)
    kernel = jnp.einsum("prsam,ka->prskm", core_cols, x_factor, precision=highest)
    mixed_re = jnp.einsum("rskm,rkm->skm", kernel[0], amplitude[0], precision=highest) - jnp.einsum(
        "rskm,rkm->skm", kernel[1], amplitude[1], precision=highest
    )
    mixed_im = jnp.einsum("rskm,rkm->skm", kernel[0], amplitude[1], precision=highest) + jnp.einsum(
        "rskm,rkm->skm", kernel[1], amplitude[0], precision=highest
    )
    mixed_sum = taken_together(jnp.stack([mixed_re, mixed_im]), "col")
    out_spec = jnp.einsum("os,qskm->qokm", out_factor, mixed_sum, precision=highest)
    x_backward = phase_table(jnp.arange(grid_x, dtype=jnp.int32), grid_x, modes_x, -1.0)
    x_values = jnp.einsum("pckm,xpqk->qcxm", out_spec, x_backward, precision=highest)
    returned = lax.all_to_all(x_values, "gx", split_axis=2, concat_axis=3, tiled=True)
    returned = returned.reshape(2, channels, planes, modes_y, modes_z)
    y_backward = phase_table(jnp.arange(grid_y, dtype=jnp.int32), grid_y, modes_y, -1.0)
    y_values = jnp.einsum("pcxjl,ypqj->cxqly", returned, y_backward, precision=highest)
    result = jnp.einsum("cxqly,qlz->cxyz", y_values, z_backward, precision=highest)
    return result.astype(jnp.bfloat16)


def solution(mesh):
    return jax.shard_map(
        per_device,
        mesh=mesh,
        in_specs=(
            P("col", "gx", None, None),
            P(None, "col", None, None, None, None),
            P("col", None),
            P("col", None),
            P(),
            P(),
            P(),
            P(),
        ),
        out_specs=P("col", "gx", None, None),
        check_vma=False,
    )
```

profile of v0, /device:TPU:1, one launch (start us, length us, event | category | flops | bytes accessed | tf_op | source)
XLA Modules:
  0.0 128.0 jit_solution(12711231185510852185)
XLA Ops:
  0.1 0.2 fusion.38
  0.3 6.5 %fusion = f32[2,16,16,4,256]{4,1,0,3,2:T(8,128)S(1)} fusion(bf16[16,4,256,128]{3,2,1,0:T(8,128)(2,1)} %param.8, f32[128,1,16]{0,2,1:T(8,128)S(1)} %get-tuple-element.26, f32[128,1,16]{0,2,1:T(8,128)S(1)} %get-tuple-element.27), kind=kOutput, calls=%fused_computation.1 | convolution fusion | flops 805310464 | bytes 6307840 | tf_op jit(solution)/shard_map/cxyz,zpl->cxply/dot_general | solution.py:77
  6.9 1.8 %fusion.5 = f32[2,16,4,32,16]{3,4,2,1,0:T(8,128)S(1)} fusion(f32[2,16,16,4,256]{4,1,0,3,2:T(8,128)S(1)} %fusion, f32[256,1,2,32]{0,3,1,2:T(8,128)S(1)} %get-tuple-element.14, f32[256,1,2,32]{0,3,1,2:T(8,128)S(1)} %get-tuple-element.15), kind=kOutput, calls=%fused_computation.8 | convolution fusion | flops 402685952 | bytes 2490368 | tf_op jit(solution)/shard_map/cxply,ypqj->qcxjl/dot_general | solution.py:78
  8.7 2.7 %copy.109 = f32[2,16,4,32,16]{1,2,0,4,3:T(4,128)} copy(f32[2,16,4,32,16]{3,4,2,1,0:T(8,128)S(1)} %fusion.5) | data formatting | bytes 524288 | tf_op jit(solution)/shard_map/reshape | solution.py:79
  11.4 3.8 %reshape.509 = f32[64,1,1024]{2,1,0:T(1,128)} reshape(f32[512,2,4,16]{3,2,1,0:T(4,128)} %bitcast.186) | data formatting | bytes 524288
  15.2 13.1 %all-to-all-start = ((f32[64,1,1024]{2,1,0:T(1,128)}), f32[64,1,1024]{2,1,0:T(1,128)S(1)}, u32[]{:S(2)}, u32[]{:S(2)}) async-start(f32[64,1,1024]{2,1,0:T(1,128)} %reshape.509), calls=%async_computation | async-start | bytes 524288 | tf_op jit(solution)/shard_map/all_to_all | solution.py:83
  28.3 0.2 fusion.57
  28.5 0.2 fusion.56
  28.7 0.1 copy.49
  28.8 0.1 reshape.478
  28.9 0.1 dynamic_slice.3
  29.0 2.6 %convolution_bitcast_fusion.1 = f32[2,8,32,8,8]{2,4,3,1,0:T(8,128)S(1)} fusion(f32[2,8,32,8,8,4]{2,5,4,3,1,0:T(4,128)S(1)} %copy-done, f32[8,8]{0,1:T(8,128)S(1)} %fusion.57, f32[8,4]{0,1:T(4,128)S(1)} %fusion.56), kind=kOutput, calls=%fused_computation.9 | convolution fusion | flops 12583168 | bytes 655744 | tf_op jit(solution)/shard_map/prsabe,mb,me->prsam/dot_general | solution.py:97
  31.6 4.8 %convolution_bitcast_fusion = f32[2,8,32,32,8]{3,2,4,1,0:T(8,128)} fusion(f32[2,8,32,8,8]{2,4,3,1,0:T(8,128)S(1)} %convolution_bitcast_fusion.1, f32[32,8]{0,1:T(8,128)S(1)} %copy-done.4), kind=kOutput, calls=%fused_computation.7 | convolution fusion | flops 12582912 | bytes 656384 | tf_op jit(solution)/shard_map/prsam,ka->prskm/dot_general | solution.py:98
  36.4 3.9 %all-to-all-done = f32[64,1,1024]{2,1,0:T(1,128)S(1)} async-done(((f32[64,1,1024]{2,1,0:T(1,128)}), f32[64,1,1024]{2,1,0:T(1,128)S(1)}, u32[]{:S(2)}, u32[]{:S(2)}) %all-to-all-start) | async-done | bytes 262176 | tf_op jit(solution)/shard_map/all_to_all | solution.py:83
  40.2 0.5 broadcast.688
  40.8 1.2 reduce.8
  42.0 2.8 %reshape.510 = f32[512,2,4,16]{3,2,1,0:T(4,128)} reshape(f32[64,1024]{1,0:T(8,128)S(1)} %reduce.8) | data formatting | bytes 524288
  44.8 2.0 %copy.133 = f32[2,16,4,512]{1,3,2,0:T(8,128)S(1)} copy(f32[2,16,4,512]{1,2,0,3:T(4,128)} %bitcast.188) | data formatting | bytes 524288 | tf_op jit(solution)/shard_map/all_to_all | solution.py:83
  46.8 1.6 %copy.44 = f32[2,16,64,4,8]{1,4,3,2,0:T(8,128)} copy(f32[2,16,64,4,8]{1,4,2,3,0:T(8,128)S(1)} %bitcast.189) | data formatting | bytes 524288 | tf_op jit(solution)/shard_map/all_to_all | solution.py:83
  48.5 2.2 %copy.45 = f32[2,16,256,8]{2,1,0,3:T(8,128)S(1)} copy(f32[2,16,256,8]{1,3,2,0:T(8,128)} %bitcast.190) | data formatting | bytes 524288 | tf_op jit(solution)/shard_map/all_to_all | solution.py:83
  50.6 0.5 convolution_bitcast_fusion.4
  51.1 0.6 convolution_bitcast_fusion.3
  51.8 0.1 copy.46
  51.9 0.8 reshape.511
  52.7 4.2 %all-to-all-start.1 = ((f32[4,1,4096]{2,1,0:T(1,128)}), f32[4,1,4096]{2,1,0:T(1,128)S(1)}, u32[]{:S(2)}, u32[]{:S(2)}) async-start(f32[4,1,4096]{2,1,0:T(1,128)} %reshape.511), calls=%async_computation.1 | async-start | bytes 131072 | tf_op jit(solution)/shard_map/all_to_all | solution.py:17
  57.0 4.4 %all-to-all-done.1 = f32[4,1,4096]{2,1,0:T(1,128)S(1)} async-done(((f32[4,1,4096]{2,1,0:T(1,128)}), f32[4,1,4096]{2,1,0:T(1,128)S(1)}, u32[]{:S(2)}, u32[]{:S(2)}) %all-to-all-start.1) | async-done | bytes 65568 | tf_op jit(solution)/shard_map/all_to_all | solution.py:17
  61.4 0.8 reduce.9
  62.2 0.1 reshape.512
  62.4 2.1 %multiply_reduce_fusion.3 = (f32[32,8,32]{0,2,1:T(8,128)S(1)}, f32[32,8,32]{0,2,1:T(8,128)S(1)}, f32[32,8,32]{0,2,1:T(8,128)S(1)}, f32[32,8,32]{0,2,1:T(8,128)S(1)}) fusion(f32[2,8,32,32,8]{3,2,4,1,0:T(8,128)} %convolution_bitcast_fusion, f32[32,8,8]{0,1,2:T(8,128)S(1)} %get-tuple-element.12, f32[32,8,8]{0,1,2:T(8,128)S(1)} %get-tuple-element.11), kind=kLoop, calls=%fused_computation.21 | loop fusion | flops 491520 | bytes 671744
  64.4 0.2 fusion.18
  64.6 0.2 fusion.17
  64.8 0.5 reshape.513
  65.3 7.9 %all_to_all.43 = f32[4,1,16384]{2,1,0:T(1,128)S(1)} all-to-all(f32[4,1,16384]{2,1,0:T(1,128)S(1)} %reshape.513), channel_id=1, replica_groups=mesh['gx'=64,'col'=4] {'col'}, dimensions={0} | all-to-all | bytes 524288 | tf_op jit(solution)/shard_map/all_to_all | solution.py:23
  73.2 1.3 %reduce.10 = f32[4,16384]{1,0:T(4,128)S(1)} reduce(f32[4,1,16384]{2,1,0:T(1,128)S(1)} %all_to_all.43, f32[]{:T(128)} %broadcast.688), dimensions={1}, to_apply=%all_to_all.35.reduce_sub_computation | reduce | bytes 524292 | tf_op jit(solution)/shard_map/all_to_all | solution.py:23
  74.6 0.3 reshape.514
  75.0 0.3 convolution_bitcast_fusion.5
  75.3 0.4 convolution_bitcast_fusion.2
  75.7 2.4 %copy.54 = f32[2,16,256,8]{1,3,0,2:T(8,128)} copy(f32[2,16,256,8]{2,1,3,0:T(8,128)S(1)} %convolution_bitcast_fusion.2) | data formatting | bytes 524288 | tf_op jit(solution)/shard_map/pckm,xpqk->qcxm/transpose | solution.py:108
  78.2 3.0 %reshape.515 = f32[64,1,1024]{2,1,0:T(1,128)} reshape(f32[256,2,8,16]{3,2,1,0:T(8,128)} %bitcast.187) | data formatting | bytes 524288
  81.2 9.0 %all-to-all-start.3 = ((f32[64,1,1024]{2,1,0:T(1,128)}), f32[64,1,1024]{2,1,0:T(1,128)S(1)}, u32[]{:S(2)}, u32[]{:S(2)}) async-start(f32[64,1,1024]{2,1,0:T(1,128)} %reshape.515), calls=%async_computation.3 | async-start | bytes 524288 | tf_op jit(solution)/shard_map/all_to_all | solution.py:109
  90.2 0.1 cosine_multiply_fusion.1
  90.3 11.9 %all-to-all-done.3 = f32[64,1,1024]{2,1,0:T(1,128)S(1)} async-done(((f32[64,1,1024]{2,1,0:T(1,128)}), f32[64,1,1024]{2,1,0:T(1,128)S(1)}, u32[]{:S(2)}, u32[]{:S(2)}) %all-to-all-start.3) | async-done | bytes 262176 | tf_op jit(solution)/shard_map/all_to_all | solution.py:109
  102.2 1.2 reduce.11
  103.4 2.0 %reshape.516 = f32[256,2,8,16]{3,2,1,0:T(8,128)} reshape(f32[64,1024]{1,0:T(8,128)S(1)} %reduce.11) | data formatting | bytes 524288
  105.5 3.1 %copy.56 = f32[2,16,4,64,8]{1,4,3,2,0:T(8,128)} copy(f32[2,16,4,64,8]{1,4,0,2,3:T(8,128)} %bitcast.191) | data formatting | bytes 524288 | tf_op jit(solution)/shard_map/all_to_all | solution.py:109
  108.5 2.7 %copy.101 = f32[2,16,4,32,16,1]{3,4,0,5,2,1:T(8,128)S(1)} copy(f32[2,16,4,32,16,1]{1,4,3,2,0,5:T(8,128)} %bitcast.192) | data formatting | bytes 524288 | tf_op jit(solution)/shard_map/reshape | solution.py:110
  111.3 1.8 %fusion.8 = f32[256,2,16,4,16,1]{0,4,1,5,3,2:T(8,128)S(1)} fusion(f32[2,16,4,32,16,1]{3,4,0,5,2,1:T(8,128)S(1)} %copy.101, f32[256,1,2,32]{0,3,2,1:T(8,128)S(1)} %get-tuple-element.16, f32[256,1,2,32]{0,3,2,1:T(8,128)S(1)} %get-tuple-element.13), kind=kOutput, calls=%fused_computation.16 | convolution fusion | flops 402685952 | bytes 2490368 | tf_op jit(solution)/shard_map/pcxjl,ypqj->cxqly/dot_general | solution.py:112
  113.1 14.9 %bitcast_convert_fusion = bf16[16,4,256,128]{3,2,1,0:T(8,128)(2,1)} fusion(f32[256,2,16,4,16,1]{0,4,1,5,3,2:T(8,128)S(1)} %fusion.8, f32[1,16,128]{2,1,0:T(8,128)S(1)} %get-tuple-element.18, f32[1,16,128]{2,1,0:T(8,128)S(1)} %get-tuple-element.17), kind=kOutput, calls=%fused_computation | convolution fusion | flops 807407616 | bytes 6307840 | tf_op jit(solution)/shard_map/cxqly,qlz->cxyz/dot_general | solution.py:113
  (28 shorter events, 0.4 us)
Async XLA Ops:
  0.0 29.0 %copy-start = (f32[2,8,32,8,8,4]{2,5,4,3,1,0:T(4,128)S(1)}, f32[2,8,32,8,8,4]{2,5,4,3,1,0:T(4,128)}, u32[]{:S(2)}) copy-start(f32[2,8,32,8,8,4]{2,5,4,3,1,0:T(4,128)} %param.9) | copy-start | bytes 1572868
  11.3 17.0 %copy-start.5 = (f32[32,8]{0,1:T(8,128)S(1)}, f32[32,8]{0,1:T(8,128)}, u32[]{:S(2)}) copy-start(f32[32,8]{0,1:T(8,128)} %param.13) | copy-start | bytes 3076
  11.3 17.2 %copy-start.6 = (f32[16,4]{0,1:T(4,128)S(1)}, f32[16,4]{0,1:T(4,128)}, u32[]{:S(2)}) copy-start(f32[16,4]{0,1:T(4,128)} %param.14) | copy-start | bytes 772
  11.3 17.4 %copy-start.1 = (s32[32,16]{0,1:T(8,128)S(1)}, s32[32,16]{0,1:T(8,128)}, u32[]{:S(2)}) copy-start(s32[32,16]{0,1:T(8,128)} %param.15) | copy-start | bytes 6148
  15.2 16.4 %copy-start.4 = (f32[32,8]{0,1:T(8,128)S(1)}, f32[32,8]{0,1:T(8,128)}, u32[]{:S(2)}) copy-start(f32[32,8]{0,1:T(8,128)} %param.12) | copy-start | bytes 3076
  15.2 25.1 %all-to-all-start = ((f32[64,1,1024]{2,1,0:T(1,128)}), f32[64,1,1024]{2,1,0:T(1,128)S(1)}, u32[]{:S(2)}, u32[]{:S(2)}) async-start(f32[64,1,1024]{2,1,0:T(1,128)} %reshape.509), calls=%async_computation | async-start | bytes 524288 | tf_op jit(solution)/shard_map/all_to_all | solution.py:83
  48.5 2.7 %copy-start.2 = (f32[16,32]{1,0:T(8,128)S(1)}, f32[16,32]{1,0:T(8,128)}, u32[]{:S(2)}) copy-start(f32[16,32]{1,0:T(8,128)} %param.10) | copy-start | bytes 6148
  52.7 8.7 %all-to-all-start.1 = ((f32[4,1,4096]{2,1,0:T(1,128)}), f32[4,1,4096]{2,1,0:T(1,128)S(1)}, u32[]{:S(2)}, u32[]{:S(2)}) async-start(f32[4,1,4096]{2,1,0:T(1,128)} %reshape.511), calls=%async_computation.1 | async-start | bytes 131072 | tf_op jit(solution)/shard_map/all_to_all | solution.py:17
  65.3 9.7 %copy-start.3 = (f32[16,32]{1,0:T(8,128)S(1)}, f32[16,32]{1,0:T(8,128)}, u32[]{:S(2)}) copy-start(f32[16,32]{1,0:T(8,128)} %param.11) | copy-start | bytes 6148
  81.2 21.0 %all-to-all-start.3 = ((f32[64,1,1024]{2,1,0:T(1,128)}), f32[64,1,1024]{2,1,0:T(1,128)S(1)}, u32[]{:S(2)}, u32[]{:S(2)}) async-start(f32[64,1,1024]{2,1,0:T(1,128)} %reshape.515), calls=%async_computation.3 | async-start | bytes 524288 | tf_op jit(solution)/shard_map/all_to_all | solution.py:109
where the time goes:
time: 129 us; the launch traced here: 128 us
  matrix products  34.6 us (27%)
  local copies, waits for them, and re-layouts  31.1 us (24%)
  starting transfers between devices  26.3 us (20%)
  waiting for transfers between devices  20.1 us (16%)
  blocking collectives  7.92 us (6%)
  other arithmetic  7.52 us (6%)
    dot_general x1, matrix products, per_device(): jnp.einsum('cxqly,qlz->cxyz', y_values, z_backward, precision=highest)  14.9 us
    unnamed x25, local copies, waits for them, and re-layouts  13.6 us
    all_to_all x1, starting transfers between devices, per_device(): lax.all_to_all(y_spectrum, 'gx', split_axis=3, concat_axis=2, tiled=True)  13.1 us
    all_to_all x1, waiting for transfers between devices, per_device(): lax.all_to_all(x_values, 'gx', split_axis=2, concat_axis=3, tiled=True)  11.9 us
    all_to_all x1, starting transfers between devices, per_device(): lax.all_to_all(x_values, 'gx', split_axis=2, concat_axis=3, tiled=True)  9.04 us
    all_to_all x1, blocking collectives, copy_for_each(): lax.all_to_all(jnp.broadcast_to(shard[None], (devices, *shard.shape)), ax...  7.92 us
    dot_general x1, matrix products, per_device(): jnp.einsum('cxyz,zpl->cxply', values, z_forward, precision=highest)  6.53 us
    all_to_all x4, local copies, waits for them, and re-layouts, per_device(): lax.all_to_all(y_spectrum, 'gx', split_axis=3, concat_axis=2, tiled=True)  6.33 us
  transfers between devices with their start and end apart: 3, of which 3 were waited for; matrix products, arithmetic and copies ran while one was open for 6% of the time, Pallas kernels for 0%

commit v1 on v0

v1 whole, which is shorter than its diff:
```python
import functools
import math

import jax
import jax.numpy as jnp
import ml_dtypes
import numpy as np
from jax import lax
from jax.experimental import pallas as pl
from jax.experimental.pallas import tpu as pltpu
from jax.sharding import PartitionSpec as P

F32 = jnp.float32
BF16 = jnp.bfloat16
FREQ_ROWS = 18
ROWS = 40


def halves(table):
    table = table.astype(np.float32)
    high = table.astype(ml_dtypes.bfloat16)
    low = (table - high.astype(np.float32)).astype(ml_dtypes.bfloat16)
    return high, low


def split(values):
    high = values.astype(BF16)
    low = (values - high.astype(F32)).astype(BF16)
    return high, low


def dot(left, right):
    return jnp.dot(left, right, preferred_element_type=F32)


def dot3(left, right):
    lh, ll = split(left)
    rh, rl = split(right)
    return dot(lh, rh) + dot(lh, rl) + dot(ll, rh)


@functools.cache
def y_forward_table():
    y = np.arange(256)[None, :]
    j = np.arange(17)[:, None]
    angle = 2 * np.pi / 256 * (y * j % 256)
    table = np.zeros((ROWS, 256))
    table[:17] = np.cos(angle) / 16
    table[FREQ_ROWS : FREQ_ROWS + 17] = np.sin(angle) / 16
    high, low = halves(table)
    return np.concatenate([high, low], 0)


@functools.cache
def y_inverse_table():
    y = np.arange(256)[:, None]
    j = np.arange(17)[None, :]
    angle = 2 * np.pi / 256 * (y * j % 256)
    table = np.zeros((256, ROWS))
    table[:, :17] = np.cos(angle) / 16
    table[:, FREQ_ROWS : FREQ_ROWS + 17] = -np.sin(angle) / 16
    high, low = halves(table)
    rest = np.zeros((256, 128 - 3 * ROWS), ml_dtypes.bfloat16)
    return np.concatenate([high, low, high, rest], 1)


def z_angles():
    z = np.arange(128)[None, :]
    kz = np.arange(16)[:, None]
    angle = 2 * np.pi / 128 * (z * kz % 128)
    scale = 1 / math.sqrt(128)
    return np.cos(angle) * scale, np.sin(angle) * scale


@functools.cache
def z_forward_table():
    c, s = z_angles()
    table = np.zeros((2, 16, 2, 2, 128))
    for sign_at, sign in ((0, 1.0), (1, -1.0)):
        table[sign_at, :, 0, 0] = c
        table[sign_at, :, 0, 1] = -sign * s
        table[sign_at, :, 1, 0] = -s
        table[sign_at, :, 1, 1] = -sign * c
    high, low = halves(table.reshape(64, 256))
    return np.concatenate([high, low], 0)


@functools.cache
def z_inverse_table():
    c, s = z_angles()
    tables = []
    for pick in range(2):
        table = np.zeros((2, 2, 16, 2, 2, 128))
        for sign_at, sign in ((0, 1.0), (1, -1.0)):
            table[sign_at, pick, :, 0, 0] = c
            table[sign_at, pick, :, 1, 0] = -s
            table[sign_at, pick, :, 0, 1] = sign * s
            table[sign_at, pick, :, 1, 1] = sign * c
        high, low = halves(table.reshape(128, 256))
        tables.append(np.concatenate([high, low, high], 0))
    return np.stack(tables)


def x_angles():
    x = np.arange(256).reshape(64, 4)
    k = np.arange(32)
    freq = np.where(k < 16, k, k - 32)
    angle = 2 * np.pi / 256 * (x[:, :, None] * freq % 256)
    return np.cos(angle) / 16, np.sin(angle) / 16


@functools.cache
def x_forward_table():
    c, s = x_angles()
    table = np.zeros((4, 2, 32, 64, 2))
    table[:, 0, :, :, 0] = c.transpose(1, 2, 0)
    table[:, 0, :, :, 1] = s.transpose(1, 2, 0)
    table[:, 1, :, :, 0] = -s.transpose(1, 2, 0)
    table[:, 1, :, :, 1] = c.transpose(1, 2, 0)
    high, low = halves(table.reshape(256, 128))
    return np.concatenate([high, low, high], 1)


@functools.cache
def x_inverse_table():
    c, s = x_angles()
    table = np.zeros((64, 2, 4, 2, 32))
    table[:, 0, :, 0] = c
    table[:, 0, :, 1] = -s
    table[:, 1, :, 0] = s
    table[:, 1, :, 1] = c
    high, low = halves(table.reshape(128, 256))
    return np.concatenate([high, low, high], 1)


CHUNKS = 8


def forward_kernel(grid_ref, ty_ref, tz_ref, send_ref, stage, lines, arrive):
    count = stage.shape[0]
    per_chunk = count // CHUNKS

    def chunk_copy(n):
        part = pl.ds(n * per_chunk, per_chunk)
        return pltpu.make_async_copy(grid_ref.at[part], stage.at[part], arrive.at[n])

    for n in range(CHUNKS):
        chunk_copy(n).start()
    table = ty_ref[...]
    for n in range(CHUNKS):
        chunk_copy(n).wait()
        for at in range(n * per_chunk, (n + 1) * per_chunk, 2):
            both = jnp.concatenate([stage[at], stage[at + 1]], axis=1)
            out = dot(table, both)
            out = out[:ROWS] + out[ROWS:]
            lines[pl.ds(at, ROWS, stride=count), :] = out[:, :128]
            lines[pl.ds(at + 1, ROWS, stride=count), :] = out[:, 128:]
    tz = tz_ref[...]
    tz_high = tz[:64]
    contract = (((1,), (1,)), ((), ()))
    pieces = []
    for p in range(9):
        at = p * 128
        values = jnp.concatenate(
            [lines[at : at + 128, :], lines[FREQ_ROWS * count + at : FREQ_ROWS * count + at + 128, :]],
            axis=1,
        )
        high, low = split(values)
        first = lax.dot_general(tz, high, contract, preferred_element_type=F32)
        second = lax.dot_general(tz_high, low, contract, preferred_element_type=F32)
        pieces.append(first[:64] + first[64:] + second)
    lane = lax.broadcasted_iota(jnp.int32, (32, 128), 1)
    for p in range(8):
        send_ref[p * 32 : (p + 1) * 32, :] = pieces[p][:32]
        if p > 0:
            send_ref[256 + p * 32 : 256 + (p + 1) * 32, :] = pieces[p][32:]
    send_ref[256:288, :] = jnp.where(lane < 64, pieces[8][32:], pieces[0][32:])


def middle_kernel(
    got_ref, tx_ref, win_ref, scale_ref, core_ref, wout_ref, vx_ref, send_ref
):
    tx = tx_ref[...]
    lane = lax.broadcasted_iota(jnp.int32, (64, 128), 1)
    waves = []
    for pair in range(2):
        cols = [got_ref[(2 * pair + n) * 128 : (2 * pair + n + 1) * 128, :] for n in range(2)]
        high, low = split(jnp.concatenate(cols, axis=1))
        out = dot(tx, jnp.concatenate([high, high, low], axis=0))
        for n in range(2):
            part = out[:, n * 128 : (n + 1) * 128]
            picked = part[:64]
            for x in range(1, 4):
                picked = jnp.where(lane % 4 == x, part[x * 64 : (x + 1) * 64], picked)
            waves.append(picked)
    amplitude = dot3(jnp.concatenate(waves, axis=1), win_ref[...])
    scaled = []
    for h in range(2):
        scale = scale_ref[h]
        scaled.append(amplitude * jnp.concatenate([scale, scale], axis=0))
    left = jnp.concatenate(
        [
            jnp.concatenate([scaled[h][:, m * 128 : (m + 1) * 128] for h in range(2)], axis=1)
            for m in range(2)
        ],
        axis=0,
    )
    core = jnp.concatenate(
        [core_ref[c, a * 8 : (a + 1) * 8, :] for a in range(8) for c in range(4)], axis=0
    )
    mixed = dot3(left, core)
    column = lane[:32] // 32 % 2
    real = jnp.where(column == 0, mixed[0:32], mixed[64:96])
    imag = jnp.where(column == 0, mixed[32:64], mixed[96:128])
    first = lane[:32] < 64
    rows = jnp.concatenate([jnp.where(first, real, imag), jnp.where(first, imag, -real)], axis=0)
    spectra = dot3(rows, wout_ref[...])
    high, low = split(spectra)
    vx = vx_ref[...]
    for pair in range(2):
        sides = []
        for n in range(2):
            at = (2 * pair + n) * 128
            zero = jnp.zeros((64, 128), F32)
            tiles = [
                [
                    jnp.where(lane % 4 == x, values[:, at : at + 128].astype(F32), zero)
                    for x in range(4)
                ]
                for values in (high, low)
            ]
            sides.append(jnp.concatenate(tiles[0] + tiles[0] + tiles[1], axis=0).astype(BF16))
        out = dot(vx, jnp.concatenate(sides, axis=1))
        for n in range(2):
            at = (2 * pair + n) * 128
            send_ref[at : at + 128, :] = out[:, n * 128 : (n + 1) * 128]


def inverse_kernel(got_ref, tz_ref, vy_ref, out_ref, lines, stage, leave):
    count = stage.shape[0]
    per_chunk = count // CHUNKS
    lines[2 * FREQ_ROWS * count :, :] = jnp.zeros(
        ((ROWS - 2 * FREQ_ROWS) * count, 128), F32
    )
    row = lax.broadcasted_iota(jnp.int32, (128, 128), 0)
    lane = lax.broadcasted_iota(jnp.int32, (128, 128), 1)

    def emit(p, values, pick):
        high, low = split(values)
        out = dot(jnp.concatenate([high, high, low], axis=1), tz_ref[pick])
        lines[p * 128 : (p + 1) * 128, :] = out[:, :128]
        at = FREQ_ROWS * count + p * 128
        lines[at : at + 128, :] = out[:, 128:]

    for t in range(4):
        block = jnp.concatenate(
            [got_ref[t * 64 : (t + 1) * 64, :], got_ref[256 + t * 64 : 256 + (t + 1) * 64, :]],
            axis=0,
        )
        turned = block.T
        for pick in range(2):
            if t == 0 and pick == 0:
                emit(0, jnp.where((row < 64) & (lane >= 64), 0.0, turned), 0)
                emit(8, jnp.where((row < 64) & (lane >= 64), turned, 0.0), 0)
            else:
                emit(2 * t + pick, turned, pick)

    def chunk_copy(n):
        part = pl.ds(n * per_chunk, per_chunk)
        return pltpu.make_async_copy(stage.at[part], out_ref.at[part], leave.at[n])

    vy = vy_ref[...]
    for n in range(CHUNKS):
        for at in range(n * per_chunk, (n + 1) * per_chunk, 2):
            both = jnp.concatenate(
                [
                    lines[pl.ds(at, ROWS, stride=count), :],
                    lines[pl.ds(at + 1, ROWS, stride=count), :],
                ],
                axis=1,
            )
            high = both.astype(BF16).astype(F32)
            low = both - high
            rest = jnp.zeros((128 - 3 * ROWS, 256), F32)
            right = jnp.concatenate([high, high, low, rest], axis=0).astype(BF16)
            out = dot(vy, right).astype(BF16)
            stage[at] = out[:, :128]
            stage[at + 1] = out[:, 128:]
        chunk_copy(n).start()
    for n in range(CHUNKS):
        chunk_copy(n).wait()


VMEM = pl.BlockSpec(memory_space=pltpu.VMEM)
ANY = pl.BlockSpec(memory_space=pl.ANY)


def forward_call(grid_field):
    count, grid_y, grid_z = grid_field.shape
    return pl.pallas_call(
        forward_kernel,
        out_shape=jax.ShapeDtypeStruct((512, 128), F32),
        in_specs=[ANY, VMEM, VMEM],
        out_specs=VMEM,
        scratch_shapes=[
            pltpu.VMEM((count, grid_y, grid_z), BF16),
            pltpu.VMEM((ROWS * count, 128), F32),
            pltpu.SemaphoreType.DMA((CHUNKS,)),
        ],
        name="forward_yz",
    )(grid_field, y_forward_table(), z_forward_table())


def middle_call(got, win, scale, core, wout):
    return pl.pallas_call(
        middle_kernel,
        out_shape=jax.ShapeDtypeStruct((512, 128), F32),
        in_specs=[VMEM] * 7,
        out_specs=VMEM,
        name="mix_columns",
    )(got, x_forward_table(), win, scale, core, wout, x_inverse_table())


def inverse_call(got, count, grid_y, grid_z):
    return pl.pallas_call(
        inverse_kernel,
        out_shape=jax.ShapeDtypeStruct((count, grid_y, grid_z), BF16),
        in_specs=[VMEM] * 3,
        out_specs=ANY,
        scratch_shapes=[
            pltpu.VMEM((ROWS * count, 128), F32),
            pltpu.VMEM((count, grid_y, grid_z), BF16),
            pltpu.SemaphoreType.DMA((CHUNKS,)),
        ],
        name="inverse_yz",
    )(got, z_inverse_table(), y_inverse_table())


def in_slot_pairs(table):
    return jnp.concatenate([table[:16], table[16:17], table[31:32], table[17:31][::-1]], axis=0)


def swap_over_col(pieces, axis):
    devices = lax.axis_size(axis)
    here = lax.axis_index(axis)
    arrived = [lax.dynamic_slice_in_dim(pieces, here, 1)]
    for step in range(1, devices):
        ring = [(n, (n + step) % devices) for n in range(devices)]
        leaving = lax.dynamic_slice_in_dim(pieces, (here + step) % devices, 1)
        arrived.append(lax.ppermute(leaving, axis, ring))
    order = [arrived[n] for n in (3, 2, 1, 0, 3, 2, 1)]
    return lax.dynamic_slice_in_dim(jnp.concatenate(order, axis=0), devices - 1 - here, devices)


def weights(core, in_factor, out_factor, x_factor, y_factor, z_factor, kx_reach, gx):
    highest = lax.Precision.HIGHEST
    group = gx // 16
    kz = gx % 16
    y_rows = in_slot_pairs(y_factor).reshape(4, 4, 2, 8)
    y_rows = lax.dynamic_slice_in_dim(y_rows, group, 1, 1)[:, 0]
    z_row = lax.dynamic_slice_in_dim(z_factor, kz, 1)[0]
    pick = y_rows[:, :, :, None] * z_row
    cols = jnp.einsum("prsabe,tmbe->tarpms", core, pick, precision=highest)
    factors = jnp.concatenate([in_factor.reshape(4, 128), out_factor.reshape(4, 128)], axis=0)
    sent = jnp.concatenate(
        [cols.reshape(4, 64, 128), jnp.broadcast_to(factors, (4, 8, 128))], axis=1
    )
    got = swap_over_col(sent, "col")
    in_full = got[:, 64:68].reshape(4, 16, 32)
    out_full = got[:, 68:72].reshape(4, 16, 32)
    same = jnp.eye(2, dtype=F32)
    win = jnp.broadcast_to(
        in_full[:, None, :, None, None, None, :]
        * same[None, :, None, None, :, None, None],
        (4, 2, 16, 4, 2, 4, 32),
    ).reshape(512, 256)
    sign = jnp.array([1.0, -1.0], F32)
    wout = jnp.broadcast_to(
        sign[:, None, None, None, None, None, None]
        * same[None, :, None, None, :, None, None]
        * jnp.transpose(out_full, (2, 0, 1))[None, None, :, :, None, :, None],
        (2, 2, 32, 4, 2, 16, 4),
    ).reshape(128, 512)
    col = lax.axis_index("col")
    reach = in_slot_pairs(kx_reach).reshape(4, 4, 2, 16)
    reach = lax.dynamic_slice(reach, (col, group, 0, kz), (1, 1, 2, 1)).reshape(2)
    slot = jnp.arange(32, dtype=jnp.int32)
    freq = jnp.abs(jnp.where(slot < 16, slot, slot - 32))
    weight = jnp.where(kz == 0, 1.0, 2.0).astype(F32)
    kept = (freq[:, None] < reach[None, :]).astype(F32) * weight
    halves_x = jnp.transpose(x_factor.reshape(32, 2, 4), (1, 0, 2))
    scale = jnp.broadcast_to(
        halves_x[:, :, None, :, None] * kept[None, :, :, None, None], (2, 32, 2, 4, 32)
    ).reshape(2, 32, 256)
    return win, scale, got[:, :64], wout


def everyone(values):
    values = values.reshape(256, 2, 128)
    return lax.all_to_all(values, ("col", "gx"), 0, 0, tiled=True).reshape(512, 128)


def per_device(
    grid_field, tucker_core, in_factor, out_factor, x_factor, y_factor, z_factor, kx_reach
):
    channels, planes, grid_y, grid_z = grid_field.shape
    count = channels * planes
    gx = lax.axis_index("gx")
    sent = forward_call(grid_field.reshape(count, grid_y, grid_z))
    got = everyone(sent)
    win, scale, core, wout = weights(
        tucker_core, in_factor, out_factor, x_factor, y_factor, z_factor, kx_reach, gx
    )
    sent = middle_call(got, win, scale, core, wout)
    got = everyone(sent)
    result = inverse_call(got, count, grid_y, grid_z)
    return result.reshape(channels, planes, grid_y, grid_z)


def solution(mesh):
    return jax.shard_map(
        per_device,
        mesh=mesh,
        in_specs=(
            P("col", "gx", None, None),
            P(None, "col", None, None, None, None),
            P("col", None),
            P("col", None),
            P(),
            P(),
            P(),
            P(),
        ),
        out_specs=P("col", "gx", None, None),
        check_vma=False,
    )
```

time: 129 us -> 77 us (0.60)
  matrix products: 34.6 us -> 2.72 us
  local copies, waits for them, and re-layouts: 31.1 us -> 9.19 us
  blocking collectives: 7.92 us -> 29.7 us
  waiting for transfers between devices: 20.1 us -> 1.06 us
  Pallas kernels: 0 us -> 12.9 us
  other arithmetic: 7.52 us -> 0.63 us
  starting transfers between devices: 26.3 us -> 20.1 us
    dot_general x12 -> x1, matrix products: 34.6 us -> 2.72 us  [weights(): cols = jnp.einsum('prsabe,tmbe->tarpms', core, pick, precision=highest)]
    all_to_all x1, blocking collectives: 7.92 us -> 29.7 us  [everyone(): lax.all_to_all(values, ('col', 'gx'), 0, 0, tiled=True).reshape(512, 128)]
    all_to_all x3 -> x1, waiting for transfers between devices: 20.1 us -> 0.01 us  [everyone(): lax.all_to_all(values, ('col', 'gx'), 0, 0, tiled=True).reshape(512, 128)]
    pallas_call x0 -> x3, Pallas kernels: none -> 12.9 us  [the longest x1 5.47 us: forward_call(): pl.pallas_call(forward_kernel, out_shape=jax.ShapeDtypeStruct((512, 128),...]
    unnamed x25 -> x26, local copies, waits for them, and re-layouts: 13.6 us -> 1 us
    all_to_all x3 -> x1, starting transfers between devices: 26.3 us -> 15.7 us  [everyone(): lax.all_to_all(values, ('col', 'gx'), 0, 0, tiled=True).reshape(512, 128)]
    all_to_all x5 -> x0, local copies, waits for them, and re-layouts: 9.41 us -> none  [the longest x4 6.33 us: per_device(): lax.all_to_all(y_spectrum, 'gx', split_axis=3, concat_axis=2, tiled=True)]
    all_to_all x4 -> x0, other arithmetic: 4.58 us -> none  [the longest x1 1.34 us: copy_for_each(): lax.all_to_all(jnp.broadcast_to(shard[None], (devices, *shard.shape)), ax...]
  transfers between devices with their start and end apart: 3 -> 4, of which waited for: 3 -> 1; matrix products, arithmetic and copies ran while one was open for 6% -> 15% of each run, Pallas kernels for 0% -> 0%
where the time goes in v1:
time: 77 us; the launch traced here: 76.7 us
  blocking collectives  29.7 us (39%)
  starting transfers between devices  20.1 us (26%)
  Pallas kernels  12.9 us (17%)
  local copies, waits for them, and re-layouts  9.19 us (12%)
  matrix products  2.72 us (4%)
  waiting for transfers between devices  1.06 us (1%)
    all_to_all x1, blocking collectives, everyone(): lax.all_to_all(values, ('col', 'gx'), 0, 0, tiled=True).reshape(512, 128)  29.7 us
    all_to_all x1, starting transfers between devices, everyone(): lax.all_to_all(values, ('col', 'gx'), 0, 0, tiled=True).reshape(512, 128)  15.7 us
    pallas_call x1, Pallas kernels, forward_call(): pl.pallas_call(forward_kernel, out_shape=jax.ShapeDtypeStruct((512, 128),...  5.47 us
    ppermute x3, starting transfers between devices, swap_over_col(): arrived.append(lax.ppermute(leaving, axis, ring))  4.41 us
    pallas_call x1, Pallas kernels, inverse_call(): pl.pallas_call(inverse_kernel, out_shape=jax.ShapeDtypeStruct((count, gri...  4.02 us
    pallas_call x1, Pallas kernels, middle_call(): pl.pallas_call(middle_kernel, out_shape=jax.ShapeDtypeStruct((512, 128),...  3.4 us
    dot_general x1, matrix products, weights(): cols = jnp.einsum('prsabe,tmbe->tarpms', core, pick, precision=highest)  2.72 us
    reshape x1, local copies, waits for them, and re-layouts, weights(): win = jnp.broadcast_to(in_full[:, None, :, None, None, None, :] * same[No...  2.09 us
  transfers between devices with their start and end apart: 4, of which 1 were waited for; matrix products, arithmetic and copies ran while one was open for 15% of the time, Pallas kernels for 0%

profile of v1, /device:TPU:1, one launch (start us, length us, event | category | flops | bytes accessed | tf_op | source)
XLA Modules:
  0.0 76.7 jit_solution(11076689521059359380)
XLA Ops:
  0.0 5.5 %forward_yz.1 = f32[512,128]{1,0:T(8,128)} custom-call(bf16[64,256,128]{2,1,0:T(8,128)(2,1)} %bitcast.33, bf16[80,256]{1,0:T(8,128)(2,1)} %constant.84.clone.ty_ref, bf16[128,256]{1,0:T(8,128)(2,1)} %constant.85.clone.tz_ref), custom_call_target="tpu_custom_call" | custom-call | tf_op jit(solution)/shard_map/forward_yz/pallas_call | solution.py:300
  5.5 15.7 %all-to-all-start = ((f32[256,2,128]{2,1,0:T(2,128)}), f32[256,2,128]{2,1,0:T(2,128)S(1)}, u32[]{:S(2)}, u32[]{:S(2)}) async-start(f32[256,2,128]{2,1,0:T(2,128)} %bitcast.34), calls=%async_computation | async-start | bytes 524288 | tf_op jit(solution)/shard_map/all_to_all | solution.py:400
  21.2 0.1 slice.33
  21.3 0.1 slice.32
  21.4 0.1 reshape.130
  21.5 0.1 reshape.131
  21.5 0.1 rev.6
  21.6 0.1 pad_maximum_fusion
  21.7 0.1 copy.47
  21.8 0.2 fusion.15
  22.0 0.0 copy-start.3
  22.0 0.0 copy-start.7
  22.0 0.0 copy-start.8
  22.0 2.7 %fusion.3 = f32[4,8,8,2,2,32]{5,0,1,2,3,4:T(4,128)S(1)} fusion(f32[2,8,32,8,8,4]{2,5,4,3,1,0:T(4,128)S(1)} %copy-done.1, f32[4]{0:T(128)S(1)} %fusion.15, f32[4,2,8]{2,0,1:T(4,128)S(1)} %copy.48), kind=kOutput, calls=%fused_computation.3 | convolution fusion | flops 12583168 | bytes 655632 | tf_op jit(solution)/shard_map/prsabe,tmbe->tarpms/dot_general | solution.py:363
  24.7 0.4 copy.50
  25.2 0.4 reshape.129
  25.6 1.4 %collective-permute-start.2 = (f32[1,72,128]{2,1,0:T(8,128)S(1)}, f32[1,72,128]{2,1,0:T(8,128)S(1)}, u32[]{:S(2)}, u32[]{:S(2)}) collective-permute-start(f32[1,72,128]{2,1,0:T(8,128)S(1)} %get-tuple-element.7), channel_id=1, source_target_pairs={{0,1},{1,2},{2,3},{3,0},{4,5},{5,6},{6,7},{7,4},{8,9},{9,10},{10,1... | collective-permute-start | bytes 110600 | tf_op jit(solution)/shard_map/ppermute | solution.py:350
  27.1 1.4 %collective-permute-start = (f32[1,72,128]{2,1,0:T(8,128)S(1)}, f32[1,72,128]{2,1,0:T(8,128)S(1)}, u32[]{:S(2)}, u32[]{:S(2)}) collective-permute-start(f32[1,72,128]{2,1,0:T(8,128)S(1)} %get-tuple-element.8), channel_id=1, source_target_pairs={{0,3},{1,0},{2,1},{3,2},{4,7},{5,4},{6,5},{7,6},{8,11},{9,8},{10,9... | collective-permute-start | bytes 110600 | tf_op jit(solution)/shard_map/ppermute | solution.py:350
  28.4 1.6 %collective-permute-start.1 = (f32[1,72,128]{2,1,0:T(8,128)S(1)}, f32[1,72,128]{2,1,0:T(8,128)S(1)}, u32[]{:S(2)}, u32[]{:S(2)}) collective-permute-start(f32[1,72,128]{2,1,0:T(8,128)S(1)} %get-tuple-element.9), channel_id=1, source_target_pairs={{0,2},{1,3},{2,0},{3,1},{4,6},{5,7},{6,4},{7,5},{8,10},{9,11},{10,... | collective-permute-start | bytes 110600 | tf_op jit(solution)/shard_map/ppermute | solution.py:350
  30.1 0.1 slice.36
  30.1 0.1 slice.37
  30.2 0.1 copy.55
  30.3 0.1 copy.60
  30.4 0.1 copy.61
  30.5 0.1 copy.59
  30.6 0.1 copy.51
  30.7 0.2 fusion.16
  30.9 0.1 compare_select_fusion
  31.0 0.1 broadcast_multiply_fusion.2
  31.1 0.1 broadcast_multiply_fusion.3
  31.1 0.2 broadcast_in_dim.10
  31.3 0.8 %reshape.135.scale_ref = f32[2,32,256]{2,1,0:T(8,128)} reshape(f32[2,32,2,4,32]{4,3,2,1,0:T(4,128)S(1)} %broadcast_in_dim.10) | data formatting | bytes 131072 | tf_op jit(solution)/shard_map/reshape | solution.py:394
  32.1 0.0 collective-permute-done
  32.1 1.1 %collective-permute-done.1 = f32[1,72,128]{2,1,0:T(8,128)S(1)} collective-permute-done((f32[1,72,128]{2,1,0:T(8,128)S(1)}, f32[1,72,128]{2,1,0:T(8,128)S(1)}, u32[]{:S(2)}, u32[]{:S(2)}) %collective-permute-start.1) | collective-permute-done | bytes 36896 | tf_op jit(solution)/shard_map/ppermute | solution.py:350
  33.3 0.1 reshape.136
  33.4 0.1 mul.102
  33.5 0.1 broadcast_multiply_fusion
  33.6 0.3 broadcast_in_dim.11
  33.9 0.8 %reshape.137 = f32[128,512]{0,1:T(8,128)S(1)} reshape(f32[2,2,32,4,2,16,4]{2,1,0,6,5,4,3:T(2,128)S(1)} %broadcast_in_dim.11) | data formatting | bytes 524288 | tf_op jit(solution)/shard_map/reshape | solution.py:383
  34.7 0.8 %copy.56.wout_ref = f32[128,512]{1,0:T(8,128)} copy(f32[128,512]{0,1:T(8,128)S(1)} %reshape.137) | data formatting | bytes 524288 | tf_op jit(solution)/shard_map/reshape | solution.py:383
  35.6 0.1 broadcast_multiply_fusion.1
  35.7 0.3 broadcast_in_dim.9
  36.0 2.1 %reshape.132.win_ref = f32[512,256]{1,0:T(8,128)} reshape(f32[4,2,16,4,2,4,32]{6,5,4,3,2,1,0:T(4,128)S(1)} %broadcast_in_dim.9) | data formatting | bytes 1048576 | tf_op jit(solution)/shard_map/reshape | solution.py:376
  38.0 0.7 constant_dynamic-slice_fusion.3.core_ref
  38.7 0.7 copy-done.2
  39.4 3.4 %mix_columns.1 = f32[512,128]{1,0:T(8,128)} custom-call(f32[512,128]{1,0:T(8,128)} %bitcast.36, bf16[256,384]{1,0:T(8,128)(2,1)} %constant.87.clone.tx_ref, f32[512,256]{1,0:T(8,128)} %reshape.132.win_ref, f32[2,32,256]{2,1,0:T(8,128)} %reshape.135.scale_ref, f32[4,64,128]{2,1,0:T(8,128)} %constant_dynamic-slice_fusion.3.core_ref, ...), custom_call_target="tpu_custom_call" | custom-call | tf_op jit(solution)/shard_map/mix_columns/pallas_call | solution.py:315
  42.8 29.7 %all_to_all.10 = f32[256,2,128]{2,1,0:T(2,128)} all-to-all(f32[256,2,128]{2,1,0:T(2,128)} %bitcast.37), channel_id=1, replica_groups=mesh['gx'=64,'col'=4] {'col','gx'}, dimensions={0} | all-to-all | bytes 524288 | tf_op jit(solution)/shard_map/all_to_all | solution.py:400
  72.5 4.0 %inverse_yz.1 = bf16[64,256,128]{2,1,0:T(8,128)(2,1)} custom-call(f32[512,128]{1,0:T(8,128)} %bitcast.35, bf16[2,384,256]{2,1,0:T(8,128)(2,1)} %constant.89.clone.tz_ref, bf16[256,128]{1,0:T(8,128)(2,1)} %constant.90.clone.vy_ref), custom_call_target="tpu_custom_call" | custom-call | tf_op jit(solution)/shard_map/inverse_yz/pallas_call | solution.py:325
  (33 shorter events, 0.2 us)
Async XLA Ops:
  0.0 21.8 %copy-start = (f32[16,4]{0,1:T(4,128)S(1)}, f32[16,4]{0,1:T(4,128)}, u32[]{:S(2)}) copy-start(f32[16,4]{0,1:T(4,128)} %param.21) | copy-start | bytes 772
  0.0 21.2 %copy-start.4 = (f32[32,8]{0,1:T(8,128)S(1)}, f32[32,8]{0,1:T(8,128)}, u32[]{:S(2)}) copy-start(f32[32,8]{0,1:T(8,128)} %param.20) | copy-start | bytes 3076
  0.0 21.4 %copy-start.5 = (f32[16,32]{1,0:T(8,128)S(1)}, f32[16,32]{1,0:T(8,128)}, u32[]{:S(2)}) copy-start(f32[16,32]{1,0:T(8,128)} %param.17) | copy-start | bytes 6148
  0.0 21.5 %copy-start.6 = (f32[16,32]{1,0:T(8,128)S(1)}, f32[16,32]{1,0:T(8,128)}, u32[]{:S(2)}) copy-start(f32[16,32]{1,0:T(8,128)} %param.18) | copy-start | bytes 6148
  0.0 22.0 %copy-start.1 = (f32[2,8,32,8,8,4]{2,5,4,3,1,0:T(4,128)S(1)}, f32[2,8,32,8,8,4]{2,5,4,3,1,0:T(4,128)}, u32[]{:S(2)}) copy-start(f32[2,8,32,8,8,4]{2,5,4,3,1,0:T(4,128)} %param.16) | copy-start | bytes 1572868
  5.5 33.2 %all-to-all-start = ((f32[256,2,128]{2,1,0:T(2,128)}), f32[256,2,128]{2,1,0:T(2,128)S(1)}, u32[]{:S(2)}, u32[]{:S(2)}) async-start(f32[256,2,128]{2,1,0:T(2,128)} %bitcast.34), calls=%async_computation | async-start | bytes 524288 | tf_op jit(solution)/shard_map/all_to_all | solution.py:400
  22.0 8.1 %copy-start.3 = (s32[32,16]{0,1:T(8,128)S(1)}, s32[32,16]{0,1:T(8,128)}, u32[]{:S(2)}) copy-start(s32[32,16]{0,1:T(8,128)} %param.22) | copy-start | bytes 6148
  22.0 8.6 %copy-start.7 = (f32[32,8]{0,1:T(8,128)S(1)}, f32[32,8]{0,1:T(8,128)}, u32[]{:S(2)}) copy-start(f32[32,8]{0,1:T(8,128)} %param.19) | copy-start | bytes 3076
  22.0 9.1 %copy-start.8 = (f32[2]{0:T(128)S(1)}, f32[2]{0:T(128)}, u32[]{:S(2)}) copy-start(f32[2]{0:T(128)} %constant.86.clone) | copy-start | bytes 28
  25.6 7.6 %collective-permute-start.2 = (f32[1,72,128]{2,1,0:T(8,128)S(1)}, f32[1,72,128]{2,1,0:T(8,128)S(1)}, u32[]{:S(2)}, u32[]{:S(2)}) collective-permute-start(f32[1,72,128]{2,1,0:T(8,128)S(1)} %get-tuple-element.7), channel_id=1, source_target_pairs={{0,1},{1,2},{2,3},{3,0},{4,5},{5,6},{6,7},{7,4},{8,9},{9,10},{10,1... | collective-permute-start | bytes 110600 | tf_op jit(solution)/shard_map/ppermute | solution.py:350
  27.1 5.1 %collective-permute-start = (f32[1,72,128]{2,1,0:T(8,128)S(1)}, f32[1,72,128]{2,1,0:T(8,128)S(1)}, u32[]{:S(2)}, u32[]{:S(2)}) collective-permute-start(f32[1,72,128]{2,1,0:T(8,128)S(1)} %get-tuple-element.8), channel_id=1, source_target_pairs={{0,3},{1,0},{2,1},{3,2},{4,7},{5,4},{6,5},{7,6},{8,11},{9,8},{10,9... | collective-permute-start | bytes 110600 | tf_op jit(solution)/shard_map/ppermute | solution.py:350
  28.4 4.8 %collective-permute-start.1 = (f32[1,72,128]{2,1,0:T(8,128)S(1)}, f32[1,72,128]{2,1,0:T(8,128)S(1)}, u32[]{:S(2)}, u32[]{:S(2)}) collective-permute-start(f32[1,72,128]{2,1,0:T(8,128)S(1)} %get-tuple-element.9), channel_id=1, source_target_pairs={{0,2},{1,3},{2,0},{3,1},{4,6},{5,7},{6,4},{7,5},{8,10},{9,11},{10,... | collective-permute-start | bytes 110600 | tf_op jit(solution)/shard_map/ppermute | solution.py:350
  38.7 0.7 copy-start.2

commit v2 on v1

--- a/solution.py
+++ b/solution.py
@@ -178,7 +178,7 @@
 
 
 def middle_kernel(
-    got_ref, tx_ref, win_ref, scale_ref, core_ref, wout_ref, vx_ref, send_ref
+    got_ref, tx_ref, sum_ref, win_ref, scale_ref, core_ref, wout_ref, spread_ref, vx_ref, send_ref
 ):
     tx = tx_ref[...]
     lane = lax.broadcasted_iota(jnp.int32, (64, 128), 1)
@@ -193,47 +193,189 @@
             for x in range(1, 4):
                 picked = jnp.where(lane % 4 == x, part[x * 64 : (x + 1) * 64], picked)
             waves.append(picked)
-    amplitude = dot3(jnp.concatenate(waves, axis=1), win_ref[...])
-    scaled = []
-    for h in range(2):
-        scale = scale_ref[h]
-        scaled.append(amplitude * jnp.concatenate([scale, scale], axis=0))
-    left = jnp.concatenate(
-        [
-            jnp.concatenate([scaled[h][:, m * 128 : (m + 1) * 128] for h in range(2)], axis=1)
-            for m in range(2)
-        ],
-        axis=0,
-    )
-    core = jnp.concatenate(
-        [core_ref[c, a * 8 : (a + 1) * 8, :] for a in range(8) for c in range(4)], axis=0
-    )
-    mixed = dot3(left, core)
+    high, low = split(jnp.concatenate(waves, axis=1))
+    spectrum = dot(jnp.concatenate([high, low], axis=0), sum_ref[...])
+    high, low = split(spectrum[:64] + spectrum[64:])
+    amplitude = dot(jnp.concatenate([high, low, high], axis=1), win_ref[...])
+    scale = scale_ref[...]
+    scaled = amplitude * jnp.concatenate([scale, scale], axis=0)
+    high, low = split(jnp.concatenate([scaled[:, :256], scaled[:, 256:]], axis=0))
+    mixed = dot(jnp.concatenate([high, low, high], axis=1), core_ref[...])
     column = lane[:32] // 32 % 2
     real = jnp.where(column == 0, mixed[0:32], mixed[64:96])
     imag = jnp.where(column == 0, mixed[32:64], mixed[96:128])
     first = lane[:32] < 64
     rows = jnp.concatenate([jnp.where(first, real, imag), jnp.where(first, imag, -real)], axis=0)
-    spectra = dot3(rows, wout_ref[...])
+    high, low = split(rows)
+    contract = (((1,), (1,)), ((), ()))
+    spectra = lax.dot_general(
+        jnp.concatenate([high, low, high], axis=1),
+        wout_ref[...],
+        contract,
+        preferred_element_type=F32,
+    )
     high, low = split(spectra)
+    both = dot(jnp.concatenate([high, low], axis=0), spread_ref[...])
     vx = vx_ref[...]
+    zero = jnp.zeros((64, 128), F32)
     for pair in range(2):
         sides = []
         for n in range(2):
             at = (2 * pair + n) * 128
-            zero = jnp.zeros((64, 128), F32)
             tiles = [
-                [
-                    jnp.where(lane % 4 == x, values[:, at : at + 128].astype(F32), zero)
-                    for x in range(4)
-                ]
-                for values in (high, low)
+                [jnp.where(lane % 4 == x, values[:, at : at + 128], zero) for x in range(4)]
+                for values in (both[:64], both[64:])
             ]
             sides.append(jnp.concatenate(tiles[0] + tiles[0] + tiles[1], axis=0).astype(BF16))
         out = dot(vx, jnp.concatenate(sides, axis=1))
         for n in range(2):
             at = (2 * pair + n) * 128
             send_ref[at : at + 128, :] = out[:, n * 128 : (n + 1) * 128]
+
+
+@functools.cache
+def sum_table():
+    table = np.zeros((4, 2, 16, 4, 2, 4, 16))
+    for m in range(2):
+        for col in range(4):
+            for c in range(16):
+                table[col, m, c, :, m, col, c] = 1
+    return table.reshape(512, 128).astype(ml_dtypes.bfloat16)
+
+
+@functools.cache
+def spread_table():
+    table = np.zeros((2, 4, 16, 4, 2, 16, 4))
+    for m in range(2):
+        for col in range(4):
+            for c in range(16):
+                table[m, col, c, col, m, c, :] = 1
+    return table.reshape(128, 512).astype(ml_dtypes.bfloat16)
+
+
+@functools.cache
+def repeat_tables():
+    ranks = np.zeros((128, 32, 8))
+    for r in range(32):
+        ranks[r, r, :] = 1
+    parts = np.zeros((2, 128, 2, 2, 32))
+    for m in range(2):
+        for s in range(32):
+            parts[m, 32 + s, 0, m, s] = 1
+            parts[m, 32 + s, 1, m, s] = -1
+    table = np.concatenate(
+        [ranks.reshape(128, 256), parts[0].reshape(128, 128), parts[1].reshape(128, 128)], 1
+    )
+    return table.astype(ml_dtypes.bfloat16)
+
+
+def repeater(rows, lanes, run):
+    row = lax.broadcasted_iota(jnp.int32, (rows, lanes), 0)
+    lane = lax.broadcasted_iota(jnp.int32, (rows, lanes), 1)
+    return (lane // run % rows == row).astype(F32)
+
+
+def exact_dot(left, right, contract=(1, 0)):
+    dims = (((contract[0],), (contract[1],)), ((), ()))
+    return lax.dot_general(
+        left, right, dims, precision=lax.Precision.HIGHEST, preferred_element_type=F32
+    )
+
+
+def slot_of(block, member):
+    p = block - 8
+    tail = jnp.where(p == 0, 16 + 15 * member, 32 - 2 * p - member)
+    return jnp.where(block < 8, 2 * block + member, tail)
+
+
+def core_kernel(
+    core_ref, y_ref, z_ref, in_ref, out_factor_ref, s0, s1, s2, s3
+):
+    gx = lax.axis_index("gx")
+    col = lax.axis_index("col")
+    row = lax.broadcasted_iota(jnp.int32, (8, 32), 0)
+    lane = lax.broadcasted_iota(jnp.int32, (8, 32), 1)
+    block = ((col + row // 2) % 4) * 4 + gx // 16
+    chosen_y = (slot_of(block, row % 2) == lane).astype(F32)
+    chosen_z = (lane[:, :16] == gx % 16).astype(F32)
+    y_rows = exact_dot(chosen_y, y_ref[...], (1, 1))
+    z_rows = exact_dot(chosen_z, z_ref[...], (1, 1))
+    pick = exact_dot(y_rows, repeater(8, 256, 4)) * exact_dot(z_rows, repeater(4, 256, 1))
+    tall = jnp.concatenate(
+        [jnp.broadcast_to(pick[n : n + 1], (8, 256)) for n in range(8)], axis=0
+    )
+    row = lax.broadcasted_iota(jnp.int32, (64, 256), 0)
+    lane = lax.broadcasted_iota(jnp.int32, (64, 256), 1)
+    tall = jnp.where(row % 8 == lane // 32, tall, 0.0)
+    high, low = split(tall)
+    both = jnp.concatenate([high, low], axis=0)
+    pad = jnp.zeros((64, 96), F32)
+    sends = (s0, s1, s2, s3)
+    for r in range(8):
+        blocks = []
+        for part in range(2):
+            at = (part * 8 + r) * 256
+            values = core_ref[at : at + 256, :]
+            right_high, right_low = split(values)
+            out = dot(both, right_high)
+            out = out[:64] + out[64:] + dot(high, right_low)
+            blocks.append(jnp.concatenate([out, pad], axis=1))
+        for t in range(4):
+            total = blocks[0][t * 16 : t * 16 + 8]
+            for part, member in ((0, 1), (1, 0), (1, 1)):
+                at = t * 16 + member * 8
+                total = total + pltpu.roll(
+                    blocks[part][at : at + 8], 64 * part + 32 * member, 1
+                )
+            sends[t][r * 8 : (r + 1) * 8, :] = total
+    factors = jnp.concatenate(
+        [in_ref[...], out_factor_ref[...], jnp.zeros((16, 64), F32)], axis=1
+    )
+    for t in range(4):
+        sends[t][64:80, :] = factors
+
+
+def weights_kernel(
+    p0, p1, p2, p3, x_ref, reach_ref, repeat_ref, win_ref, scale_ref, core_ref, wout_ref, tall
+):
+    gx = lax.axis_index("gx")
+    col = lax.axis_index("col")
+    kz = gx % 16
+    for t, piece in enumerate((p0, p1, p2, p3)):
+        source = (col - t + 4) % 4
+        high, low = split(piece[:64, :])
+        at = source * 64
+        core_ref[pl.ds(pl.multiple_of(at, 64), 64), :] = high
+        core_ref[pl.ds(pl.multiple_of(256 + at, 64), 64), :] = high
+        core_ref[pl.ds(pl.multiple_of(512 + at, 64), 64), :] = low
+        tall[pl.ds(pl.multiple_of(source * 16, 16), 16), :] = piece[64:, :]
+    high, low = split(tall[...])
+    spread = dot(jnp.concatenate([high, low], axis=0), repeat_ref[...])
+    zero = jnp.zeros((64, 256), F32)
+    tops = []
+    for values in (spread[:64, :256], spread[64:, :256]):
+        tops.append(
+            jnp.concatenate(
+                [jnp.concatenate([values, zero], axis=1), jnp.concatenate([zero, values], axis=1)],
+                axis=0,
+            ).astype(BF16)
+        )
+    win_ref[:128] = tops[0]
+    win_ref[128:256] = tops[0]
+    win_ref[256:] = tops[1]
+    outs = [
+        jnp.concatenate([values[:, 256:384], values[:, 384:]], axis=0).astype(BF16)
+        for values in (spread[:64], spread[64:])
+    ]
+    wout_ref[...] = jnp.concatenate([outs[0], outs[0], outs[1]], axis=1)
+    slot = lax.broadcasted_iota(jnp.int32, (32, 256), 0)
+    freq = jnp.where(slot < 16, slot, 32 - slot)
+    weight = jnp.where(kz == 0, 1.0, 2.0).astype(F32)
+    block = col * 4 + gx // 16
+    wide = exact_dot(x_ref[...], repeater(8, 256, 1)) * weight
+    for member in range(2):
+        reach = reach_ref[kz, slot_of(block, member)]
+        scale_ref[:, member * 256 : (member + 1) * 256] = jnp.where(freq < reach, wide, 0.0)
 
 
 def inverse_kernel(got_ref, tz_ref, vy_ref, out_ref, lines, stage, leave):
@@ -292,15 +434,21 @@
 
 
 VMEM = pl.BlockSpec(memory_space=pltpu.VMEM)
-ANY = pl.BlockSpec(memory_space=pl.ANY)
+
+
+def room(mebibytes):
+    return pltpu.CompilerParams(vmem_limit_bytes=mebibytes << 20)
+
+
+HBM = pl.BlockSpec(memory_space=pltpu.HBM)
 
 
 def forward_call(grid_field):
     count, grid_y, grid_z = grid_field.shape
     return pl.pallas_call(
         forward_kernel,
-        out_shape=jax.ShapeDtypeStruct((512, 128), F32),
-        in_specs=[ANY, VMEM, VMEM],
+        out_shape=pltpu.VMEM((512, 128), F32),
+        in_specs=[HBM, VMEM, VMEM],
         out_specs=VMEM,
         scratch_shapes=[
             pltpu.VMEM((count, grid_y, grid_z), BF16),
@@ -314,85 +462,76 @@
 def middle_call(got, win, scale, core, wout):
     return pl.pallas_call(
         middle_kernel,
-        out_shape=jax.ShapeDtypeStruct((512, 128), F32),
-        in_specs=[VMEM] * 7,
+        out_shape=pltpu.VMEM((512, 128), F32),
+        in_specs=[VMEM] * 9,
         out_specs=VMEM,
+        compiler_params=room(12),
         name="mix_columns",
-    )(got, x_forward_table(), win, scale, core, wout, x_inverse_table())
+    )(
+        got,
+        x_forward_table(),
+        sum_table(),
+        win,
+        scale,
+        core,
+        wout,
+        spread_table(),
+        x_inverse_table(),
+    )
+
+
+def core_call(core, y_factor, z_factor, in_factor, out_factor):
+    piece = pltpu.VMEM((80, 128), F32)
+    return pl.pallas_call(
+        core_kernel,
+        out_shape=(piece,) * 4,
+        in_specs=[VMEM] * 5,
+        out_specs=(VMEM,) * 4,
+        compiler_params=room(12),
+        name="contract_core",
+    )(core, y_factor.T, z_factor.T, in_factor, out_factor)
+
+
+def weights_call(pieces, x_factor, kx_reach):
+    return pl.pallas_call(
+        weights_kernel,
+        out_shape=(
+            pltpu.VMEM((384, 512), BF16),
+            pltpu.VMEM((32, 512), F32),
+            pltpu.VMEM((768, 128), BF16),
+            pltpu.VMEM((128, 384), BF16),
+        ),
+        in_specs=[VMEM] * 5 + [pl.BlockSpec(memory_space=pltpu.SMEM)] + [VMEM],
+        out_specs=(VMEM,) * 4,
+        scratch_shapes=[pltpu.VMEM((64, 128), F32)],
+        compiler_params=room(12),
+        name="build_weights",
+    )(*pieces, x_factor, kx_reach.T, repeat_tables())
 
 
 def inverse_call(got, count, grid_y, grid_z):
     return pl.pallas_call(
         inverse_kernel,
-        out_shape=jax.ShapeDtypeStruct((count, grid_y, grid_z), BF16),
+        out_shape=pltpu.HBM((count, grid_y, grid_z), BF16),
         in_specs=[VMEM] * 3,
-        out_specs=ANY,
+        out_specs=HBM,
         scratch_shapes=[
             pltpu.VMEM((ROWS * count, 128), F32),
             pltpu.VMEM((count, grid_y, grid_z), BF16),
             pltpu.SemaphoreType.DMA((CHUNKS,)),
         ],
+        compiler_params=room(16),
         name="inverse_yz",
     )(got, z_inverse_table(), y_inverse_table())
 
 
-def in_slot_pairs(table):
-    return jnp.concatenate([table[:16], table[16:17], table[31:32], table[17:31][::-1]], axis=0)
-
-
-def swap_over_col(pieces, axis):
-    devices = lax.axis_size(axis)
-    here = lax.axis_index(axis)
-    arrived = [lax.dynamic_slice_in_dim(pieces, here, 1)]
+def swap_over_col(pieces):
+    devices = lax.axis_size("col")
+    arrived = [pieces[0]]
     for step in range(1, devices):
         ring = [(n, (n + step) % devices) for n in range(devices)]
-        leaving = lax.dynamic_slice_in_dim(pieces, (here + step) % devices, 1)
-        arrived.append(lax.ppermute(leaving, axis, ring))
-    order = [arrived[n] for n in (3, 2, 1, 0, 3, 2, 1)]
-    return lax.dynamic_slice_in_dim(jnp.concatenate(order, axis=0), devices - 1 - here, devices)
-
-
-def weights(core, in_factor, out_factor, x_factor, y_factor, z_factor, kx_reach, gx):
-    highest = lax.Precision.HIGHEST
-    group = gx // 16
-    kz = gx % 16
-    y_rows = in_slot_pairs(y_factor).reshape(4, 4, 2, 8)
-    y_rows = lax.dynamic_slice_in_dim(y_rows, group, 1, 1)[:, 0]
-    z_row = lax.dynamic_slice_in_dim(z_factor, kz, 1)[0]
-    pick = y_rows[:, :, :, None] * z_row
-    cols = jnp.einsum("prsabe,tmbe->tarpms", core, pick, precision=highest)
-    factors = jnp.concatenate([in_factor.reshape(4, 128), out_factor.reshape(4, 128)], axis=0)
-    sent = jnp.concatenate(
-        [cols.reshape(4, 64, 128), jnp.broadcast_to(factors, (4, 8, 128))], axis=1
-    )
-    got = swap_over_col(sent, "col")
-    in_full = got[:, 64:68].reshape(4, 16, 32)
-    out_full = got[:, 68:72].reshape(4, 16, 32)
-    same = jnp.eye(2, dtype=F32)
-    win = jnp.broadcast_to(
-        in_full[:, None, :, None, None, None, :]
-        * same[None, :, None, None, :, None, None],
-        (4, 2, 16, 4, 2, 4, 32),
-    ).reshape(512, 256)
-    sign = jnp.array([1.0, -1.0], F32)
-    wout = jnp.broadcast_to(
-        sign[:, None, None, None, None, None, None]
-        * same[None, :, None, None, :, None, None]
-        * jnp.transpose(out_full, (2, 0, 1))[None, None, :, :, None, :, None],
-        (2, 2, 32, 4, 2, 16, 4),
-    ).reshape(128, 512)
-    col = lax.axis_index("col")
-    reach = in_slot_pairs(kx_reach).reshape(4, 4, 2, 16)
-    reach = lax.dynamic_slice(reach, (col, group, 0, kz), (1, 1, 2, 1)).reshape(2)
-    slot = jnp.arange(32, dtype=jnp.int32)
-    freq = jnp.abs(jnp.where(slot < 16, slot, slot - 32))
-    weight = jnp.where(kz == 0, 1.0, 2.0).astype(F32)
-    kept = (freq[:, None] < reach[None, :]).astype(F32) * weight
-    halves_x = jnp.transpose(x_factor.reshape(32, 2, 4), (1, 0, 2))
-    scale = jnp.broadcast_to(
-        halves_x[:, :, None, :, None] * kept[None, :, :, None, None], (2, 32, 2, 4, 32)
-    ).reshape(2, 32, 256)
-    return win, scale, got[:, :64], wout
+        arrived.append(lax.ppermute(pieces[step], "col", ring))
+    return arrived
 
 
 def everyone(values):
@@ -405,12 +544,11 @@
 ):
     channels, planes, grid_y, grid_z = grid_field.shape
     count = channels * planes
-    gx = lax.axis_index("gx")
     sent = forward_call(grid_field.reshape(count, grid_y, grid_z))
     got = everyone(sent)
-    win, scale, core, wout = weights(
-        tucker_core, in_factor, out_factor, x_factor, y_factor, z_factor, kx_reach, gx
-    )
+    core = jnp.transpose(tucker_core, (0, 1, 3, 4, 5, 2)).reshape(-1, tucker_core.shape[2])
+    pieces = core_call(core, y_factor, z_factor, in_factor, out_factor)
+    win, scale, core, wout = weights_call(swap_over_col(pieces), x_factor, kx_reach)
     sent = middle_call(got, win, scale, core, wout)
     got = everyone(sent)
     result = inverse_call(got, count, grid_y, grid_z)

time: 77 us -> 70.2 us (0.912)
  local copies, waits for them, and re-layouts: 9.19 us -> 5.09 us
  waiting for transfers between devices: 1.06 us -> 4.22 us
  matrix products: 2.72 us -> 0 us
  blocking collectives: 29.7 us -> 27.6 us
    reshape x8 -> x0, local copies, waits for them, and re-layouts: 5.24 us -> none  [the longest x1 2.09 us: weights(): win = jnp.broadcast_to(in_full[:, None, :, None, None, None, :] * same[No...]
    unnamed x26 -> x31, local copies, waits for them, and re-layouts: 1 us -> 5.09 us
    dot_general x1 -> x0, matrix products: 2.72 us -> none  [weights(): cols = jnp.einsum('prsabe,tmbe->tarpms', core, pick, precision=highest)]
    all_to_all x1, waiting for transfers between devices: 0.01 us -> 2.6 us  [everyone(): lax.all_to_all(values, ('col', 'gx'), 0, 0, tiled=True).reshape(512, 128)]
    all_to_all x1, blocking collectives: 29.7 us -> 27.6 us  [everyone(): lax.all_to_all(values, ('col', 'gx'), 0, 0, tiled=True).reshape(512, 128)]
    slice x6 -> x0, local copies, waits for them, and re-layouts: 0.98 us -> none  [the longest x1 0.67 us: weights(): return (win, scale, got[:, :64], wout)]
    pallas_call x3 -> x5, Pallas kernels: 12.9 us -> 12.3 us  [the longest x1 5.55 us: forward_call(): pl.pallas_call(forward_kernel, out_shape=pltpu.VMEM((512, 128), F32), in_...]
  transfers between devices with their start and end apart: 4 -> 4, of which waited for: 1 -> 2; matrix products, arithmetic and copies ran while one was open for 15% -> 1% of each run, Pallas kernels for 0% -> 4%
where the time goes in v2:
time: 70.2 us; the launch traced here: 69.9 us
  blocking collectives  27.6 us (39%)
  starting transfers between devices  20.6 us (29%)
  Pallas kernels  12.3 us (18%)
  local copies, waits for them, and re-layouts  5.09 us (7%)
  waiting for transfers between devices  4.22 us (6%)
    all_to_all x1, blocking collectives, everyone(): lax.all_to_all(values, ('col', 'gx'), 0, 0, tiled=True).reshape(512, 128)  27.6 us
    all_to_all x1, starting transfers between devices, everyone(): lax.all_to_all(values, ('col', 'gx'), 0, 0, tiled=True).reshape(512, 128)  15.7 us
    pallas_call x1, Pallas kernels, forward_call(): pl.pallas_call(forward_kernel, out_shape=pltpu.VMEM((512, 128), F32), in_...  5.55 us
    unnamed x31, local copies, waits for them, and re-layouts  5.09 us
    ppermute x3, starting transfers between devices, swap_over_col(): arrived.append(lax.ppermute(pieces[step], 'col', ring))  4.93 us
    pallas_call x1, Pallas kernels, inverse_call(): pl.pallas_call(inverse_kernel, out_shape=pltpu.HBM((count, grid_y, grid_z...  2.93 us
    all_to_all x1, waiting for transfers between devices, everyone(): lax.all_to_all(values, ('col', 'gx'), 0, 0, tiled=True).reshape(512, 128)  2.6 us
    ppermute x3, waiting for transfers between devices, swap_over_col(): arrived.append(lax.ppermute(pieces[step], 'col', ring))  1.62 us
  transfers between devices with their start and end apart: 4, of which 2 were waited for; matrix products, arithmetic and copies ran while one was open for 1% of the time, Pallas kernels for 4%

profile of v2, /device:TPU:1, one launch (start us, length us, event | category | flops | bytes accessed | tf_op | source)
XLA Modules:
  0.0 69.9 jit_solution(947340311836468746)
XLA Ops:
  0.0 0.0 copy-start.4
  0.0 0.0 copy-start.2
  0.0 0.0 copy-start.5
  0.0 0.0 copy-start.6
  0.0 0.0 copy-start.3
  0.0 0.0 copy-start.11
  0.0 0.0 copy-start.10
  0.1 0.0 copy-start
  0.1 0.0 copy-start.1
  0.1 5.5 %forward_yz.1 = f32[512,128]{1,0:T(8,128)} custom-call(bf16[64,256,128]{2,1,0:T(8,128)(2,1)} %bitcast.19, bf16[80,256]{1,0:T(8,128)(2,1)} %constant.18.clone.ty_ref, bf16[128,256]{1,0:T(8,128)(2,1)} %constant.19.clone.tz_ref), custom_call_target="tpu_custom_call" | custom-call | tf_op jit(solution)/shard_map/forward_yz/pallas_call | solution.py:448
  5.6 15.7 %all-to-all-start = ((f32[256,2,128]{2,1,0:T(2,128)}), f32[256,2,128]{2,1,0:T(2,128)S(1)}, u32[]{:S(2)}, u32[]{:S(2)}) async-start(f32[256,2,128]{2,1,0:T(2,128)} %bitcast.1), calls=%async_computation | async-start | bytes 524288 | tf_op jit(solution)/shard_map/all_to_all | solution.py:539
  21.3 0.0 copy-done.11
  21.3 0.0 copy-done.10
  21.3 0.0 copy-done
  21.3 0.0 copy-start.13
  21.3 0.7 copy-done.13
  22.0 0.0 copy-start.14
  22.0 0.7 copy-done.14
  22.7 1.6 %contract_core.1 = (f32[80,128]{1,0:T(8,128)S(1)}, f32[80,128]{1,0:T(8,128)}, f32[80,128]{1,0:T(8,128)}, f32[80,128]{1,0:T(8,128)}) custom-call(f32[4096,32]{1,0:T(8,128)S(1)} %bitcast.12, f32[8,32]{1,0:T(8,128)S(1)} %bitcast.17, f32[4,16]{1,0:T(4,128)S(1)} %bitcast.18, f32[16,32]{1,0:T(8,128)S(1)} %copy-done.10, f32[16,32]{1,0:T(8,128)S(1)} %copy-done.11), custom_call_target="tpu_custom_call" | custom-call | tf_op jit(solution)/shard_map/contract_core/pallas_call | solution.py:485
  24.3 0.0 copy-start.8
  24.3 0.6 copy-done.8
  24.9 1.4 %collective-permute-start = (f32[80,128]{1,0:T(8,128)}, f32[80,128]{1,0:T(8,128)S(1)}, u32[]{:S(2)}, u32[]{:S(2)}) collective-permute-start(f32[80,128]{1,0:T(8,128)} %get-tuple-element.14), channel_id=1, source_target_pairs={{0,1},{1,2},{2,3},{3,0},{4,5},{5,6},{6,7},{7,4},{8,9},{9,10},{10,1... | collective-permute-start | bytes 122888 | tf_op jit(solution)/shard_map/ppermute | solution.py:533
  26.3 2.5 %collective-permute-start.1 = (f32[80,128]{1,0:T(8,128)}, f32[80,128]{1,0:T(8,128)S(1)}, u32[]{:S(2)}, u32[]{:S(2)}) collective-permute-start(f32[80,128]{1,0:T(8,128)} %get-tuple-element.15), channel_id=1, source_target_pairs={{0,2},{1,3},{2,0},{3,1},{4,6},{5,7},{6,4},{7,5},{8,10},{9,11},{10,... | collective-permute-start | bytes 122888 | tf_op jit(solution)/shard_map/ppermute | solution.py:533
  28.7 1.1 %collective-permute-start.2 = (f32[80,128]{1,0:T(8,128)}, f32[80,128]{1,0:T(8,128)S(1)}, u32[]{:S(2)}, u32[]{:S(2)}) collective-permute-start(f32[80,128]{1,0:T(8,128)} %get-tuple-element.16), channel_id=1, source_target_pairs={{0,3},{1,0},{2,1},{3,2},{4,7},{5,4},{6,5},{7,6},{8,11},{9,8},{10,9... | collective-permute-start | bytes 122888 | tf_op jit(solution)/shard_map/ppermute | solution.py:533
  29.8 0.8 %copy.18.x_ref = f32[32,8]{1,0:T(8,128)S(1)} copy(f32[32,8]{0,1:T(8,128)} %param.21) | data formatting | bytes 2048 | tf_op args[4]
  30.6 0.0 collective-permute-done.p1
  30.6 1.6 %collective-permute-done.1.p2 = f32[80,128]{1,0:T(8,128)S(1)} collective-permute-done((f32[80,128]{1,0:T(8,128)}, f32[80,128]{1,0:T(8,128)S(1)}, u32[]{:S(2)}, u32[]{:S(2)}) %collective-permute-start.1) | collective-permute-done | bytes 40992 | tf_op jit(solution)/shard_map/ppermute | solution.py:533
  32.2 0.0 collective-permute-done.2.p3
  32.2 0.0 copy-done.4
  32.2 0.0 copy-start.9
  32.2 0.8 %copy-done.9 = f32[80,128]{1,0:T(8,128)S(1)} copy-done((f32[80,128]{1,0:T(8,128)S(1)}, f32[80,128]{1,0:T(8,128)}, u32[]{:S(2)}) %copy-start.9) | copy-done | bytes 40984
  33.0 0.0 copy-start.12
  33.0 0.7 copy-done.12
  33.7 0.9 %build_weights.1 = (bf16[384,512]{1,0:T(8,128)(2,1)S(1)}, f32[32,512]{1,0:T(8,128)S(1)}, bf16[768,128]{1,0:T(8,128)(2,1)S(1)}, bf16[128,384]{1,0:T(8,128)(2,1)S(1)}) custom-call(f32[80,128]{1,0:T(8,128)S(1)} %copy-done.9, f32[80,128]{1,0:T(8,128)S(1)} %collective-permute-done.p1, f32[80,128]{1,0:T(8,128)S(1)} %collective-permute-done.1.p2, ...), custom_call_target="tpu_custom_call" | custom-call | tf_op jit(solution)/shard_map/build_weights/pallas_call | solution.py:496
  34.6 2.6 %all-to-all-done = f32[256,2,128]{2,1,0:T(2,128)S(1)} async-done(((f32[256,2,128]{2,1,0:T(2,128)}), f32[256,2,128]{2,1,0:T(2,128)S(1)}, u32[]{:S(2)}, u32[]{:S(2)}) %all-to-all-start) | async-done | bytes 262176 | tf_op jit(solution)/shard_map/all_to_all | solution.py:539
  37.2 0.0 copy-done.2
  37.2 0.0 copy-done.5
  37.2 0.0 copy-done.6
  37.2 0.0 copy-done.3
  37.2 1.3 %mix_columns.1 = f32[512,128]{1,0:T(8,128)S(1)} custom-call(f32[512,128]{1,0:T(8,128)S(1)} %bitcast.14, bf16[256,384]{1,0:T(8,128)(2,1)S(1)} %copy-done.3, bf16[512,128]{1,0:T(8,128)(2,1)S(1)} %copy-done.6, bf16[384,512]{1,0:T(8,128)(2,1)S(1)} %get-tuple-element.17.win_ref, f32[32,512]{1,0:T(8,128)S(1)} %get-tuple-element.18.scale_ref, ...), custom_call_target="tpu_custom_call" | custom-call | tf_op jit(solution)/shard_map/mix_columns/pallas_call | solution.py:463
  38.5 27.6 %all_to_all.10 = f32[256,2,128]{2,1,0:T(2,128)S(1)} all-to-all(f32[256,2,128]{2,1,0:T(2,128)S(1)} %bitcast.15), channel_id=1, replica_groups=mesh['gx'=64,'col'=4] {'col','gx'}, dimensions={0} | all-to-all | bytes 524288 | tf_op jit(solution)/shard_map/all_to_all | solution.py:539
  66.1 0.0 copy-done.1
  66.1 0.0 copy-start.7
  66.1 0.8 %copy-done.7 = bf16[256,128]{1,0:T(8,128)(2,1)S(1)} copy-done((bf16[256,128]{1,0:T(8,128)(2,1)S(1)}, bf16[256,128]{1,0:T(8,128)(2,1)}, u32[]{:S(2)}) %copy-start.7) | copy-done | bytes 65560
  66.9 2.9 %inverse_yz.1 = bf16[64,256,128]{2,1,0:T(8,128)(2,1)} custom-call(f32[512,128]{1,0:T(8,128)S(1)} %bitcast.13, bf16[2,384,256]{2,1,0:T(8,128)(2,1)S(1)} %copy-done.1, bf16[256,128]{1,0:T(8,128)(2,1)S(1)} %copy-done.7), custom_call_target="tpu_custom_call" | custom-call | tf_op jit(solution)/shard_map/inverse_yz/pallas_call | solution.py:513
Async XLA Ops:
  0.0 32.2 %copy-start.4 = (bf16[128,512]{1,0:T(8,128)(2,1)S(1)}, bf16[128,512]{1,0:T(8,128)(2,1)}, u32[]{:S(2)}) copy-start(bf16[128,512]{1,0:T(8,128)(2,1)} %constant.20.clone.repeat_ref) | copy-start | bytes 393220
  0.0 37.2 %copy-start.2 = (bf16[128,768]{1,0:T(8,128)(2,1)S(1)}, bf16[128,768]{1,0:T(8,128)(2,1)}, u32[]{:S(2)}) copy-start(bf16[128,768]{1,0:T(8,128)(2,1)} %constant.24.clone.vx_ref) | copy-start | bytes 589828
  0.0 37.2 %copy-start.5 = (bf16[128,512]{1,0:T(8,128)(2,1)S(1)}, bf16[128,512]{1,0:T(8,128)(2,1)}, u32[]{:S(2)}) copy-start(bf16[128,512]{1,0:T(8,128)(2,1)} %constant.23.clone.spread_ref) | copy-start | bytes 393220
  0.0 37.2 %copy-start.6 = (bf16[512,128]{1,0:T(8,128)(2,1)S(1)}, bf16[512,128]{1,0:T(8,128)(2,1)}, u32[]{:S(2)}) copy-start(bf16[512,128]{1,0:T(8,128)(2,1)} %constant.22.clone.sum_ref) | copy-start | bytes 393220
  0.0 37.2 %copy-start.3 = (bf16[256,384]{1,0:T(8,128)(2,1)S(1)}, bf16[256,384]{1,0:T(8,128)(2,1)}, u32[]{:S(2)}) copy-start(bf16[256,384]{1,0:T(8,128)(2,1)} %constant.21.clone.tx_ref) | copy-start | bytes 589828
  0.0 21.3 %copy-start.11 = (f32[16,32]{1,0:T(8,128)S(1)}, f32[16,32]{1,0:T(8,128)}, u32[]{:S(2)}) copy-start(f32[16,32]{1,0:T(8,128)} %out_factor_ref.1) | copy-start | bytes 6148
  0.0 21.3 %copy-start.10 = (f32[16,32]{1,0:T(8,128)S(1)}, f32[16,32]{1,0:T(8,128)}, u32[]{:S(2)}) copy-start(f32[16,32]{1,0:T(8,128)} %in_ref.1) | copy-start | bytes 6148
  0.1 21.3 %copy-start = (f32[2,8,32,8,8,4]{2,5,4,3,1,0:T(4,128)S(1)}, f32[2,8,32,8,8,4]{2,5,4,3,1,0:T(4,128)}, u32[]{:S(2)}) copy-start(f32[2,8,32,8,8,4]{2,5,4,3,1,0:T(4,128)} %param.18) | copy-start | bytes 1572868
  0.1 66.0 %copy-start.1 = (bf16[2,384,256]{2,1,0:T(8,128)(2,1)S(1)}, bf16[2,384,256]{2,1,0:T(8,128)(2,1)}, u32[]{:S(2)}) copy-start(bf16[2,384,256]{2,1,0:T(8,128)(2,1)} %constant.25.clone.tz_ref) | copy-start | bytes 1179652
  5.6 31.6 %all-to-all-start = ((f32[256,2,128]{2,1,0:T(2,128)}), f32[256,2,128]{2,1,0:T(2,128)S(1)}, u32[]{:S(2)}, u32[]{:S(2)}) async-start(f32[256,2,128]{2,1,0:T(2,128)} %bitcast.1), calls=%async_computation | async-start | bytes 524288 | tf_op jit(solution)/shard_map/all_to_all | solution.py:539
  21.3 0.7 copy-start.13
  22.0 0.7 copy-start.14
  24.3 0.6 copy-start.8
  24.9 5.7 %collective-permute-start = (f32[80,128]{1,0:T(8,128)}, f32[80,128]{1,0:T(8,128)S(1)}, u32[]{:S(2)}, u32[]{:S(2)}) collective-permute-start(f32[80,128]{1,0:T(8,128)} %get-tuple-element.14), channel_id=1, source_target_pairs={{0,1},{1,2},{2,3},{3,0},{4,5},{5,6},{6,7},{7,4},{8,9},{9,10},{10,1... | collective-permute-start | bytes 122888 | tf_op jit(solution)/shard_map/ppermute | solution.py:533
  26.3 5.9 %collective-permute-start.1 = (f32[80,128]{1,0:T(8,128)}, f32[80,128]{1,0:T(8,128)S(1)}, u32[]{:S(2)}, u32[]{:S(2)}) collective-permute-start(f32[80,128]{1,0:T(8,128)} %get-tuple-element.15), channel_id=1, source_target_pairs={{0,2},{1,3},{2,0},{3,1},{4,6},{5,7},{6,4},{7,5},{8,10},{9,11},{10,... | collective-permute-start | bytes 122888 | tf_op jit(solution)/shard_map/ppermute | solution.py:533
  28.7 3.5 %collective-permute-start.2 = (f32[80,128]{1,0:T(8,128)}, f32[80,128]{1,0:T(8,128)S(1)}, u32[]{:S(2)}, u32[]{:S(2)}) collective-permute-start(f32[80,128]{1,0:T(8,128)} %get-tuple-element.16), channel_id=1, source_target_pairs={{0,3},{1,0},{2,1},{3,2},{4,7},{5,4},{6,5},{7,6},{8,11},{9,8},{10,9... | collective-permute-start | bytes 122888 | tf_op jit(solution)/shard_map/ppermute | solution.py:533
  32.2 0.8 %copy-start.9 = (f32[80,128]{1,0:T(8,128)S(1)}, f32[80,128]{1,0:T(8,128)}, u32[]{:S(2)}) copy-start(f32[80,128]{1,0:T(8,128)} %copy-done.8) | copy-start | bytes 122884
  33.0 0.7 copy-start.12
  66.1 0.8 %copy-start.7 = (bf16[256,128]{1,0:T(8,128)(2,1)S(1)}, bf16[256,128]{1,0:T(8,128)(2,1)}, u32[]{:S(2)}) copy-start(bf16[256,128]{1,0:T(8,128)(2,1)} %constant.26.clone.vy_ref) | copy-start | bytes 196612

commit v3 on v2

--- a/solution.py
+++ b/solution.py
@@ -136,17 +136,107 @@
 CHUNKS = 8
 
 
-def forward_kernel(grid_ref, ty_ref, tz_ref, send_ref, stage, lines, arrive):
+def column_picks(y, z, gx, col):
+    row = lax.broadcasted_iota(jnp.int32, (8, 32), 0)
+    lane = lax.broadcasted_iota(jnp.int32, (8, 32), 1)
+    block = ((col + row // 2) % 4) * 4 + gx // 16
+    chosen_y = (slot_of(block, row % 2) == lane).astype(F32)
+    chosen_z = (lane[:, :16] == gx % 16).astype(F32)
+    y_rows = exact_dot(chosen_y, y, (1, 1))
+    z_rows = exact_dot(chosen_z, z, (1, 1))
+    pick = exact_dot(y_rows, repeater(8, 256, 4)) * exact_dot(z_rows, repeater(4, 256, 1))
+    tall = jnp.concatenate(
+        [jnp.broadcast_to(pick[n : n + 1], (8, 256)) for n in range(8)], axis=0
+    )
+    row = lax.broadcasted_iota(jnp.int32, (64, 256), 0)
+    lane = lax.broadcasted_iota(jnp.int32, (64, 256), 1)
+    return split(jnp.where(row % 8 == lane // 32, tall, 0.0))
+
+
+def kept_scale(x, reach, gx, col, scale_ref):
+    kz = gx % 16
+    slot = lax.broadcasted_iota(jnp.int32, (32, 256), 0)
+    freq = jnp.where(slot < 16, slot, 32 - slot).astype(F32)
+    weight = jnp.where(kz == 0, 1.0, 2.0).astype(F32)
+    block = col * 4 + gx // 16
+    wide = exact_dot(x, repeater(8, 256, 1), (0, 0)) * weight
+    row = lax.broadcasted_iota(jnp.int32, (16, 32), 0)
+    lane = lax.broadcasted_iota(jnp.int32, (16, 32), 1)
+    for member in range(2):
+        here = (row == kz) & (lane == slot_of(block, member))
+        bound = jnp.sum(jnp.where(here, reach.astype(F32), 0.0), axis=1, keepdims=True)
+        bound = jnp.sum(bound, axis=0, keepdims=True)
+        scale_ref[:, member * 256 : (member + 1) * 256] = jnp.where(freq < bound, wide, 0.0)
+
+
+def contract_core(core, high, low, in_rows, out_rows, sends):
+    both = jnp.concatenate([high, low], axis=0)
+    pad = jnp.zeros((64, 96), F32)
+    for r in range(8):
+        blocks = []
+        for part in range(2):
+            at = (part * 8 + r) * 256
+            right_high, right_low = split(core[at : at + 256, :])
+            out = dot(both, right_high)
+            out = out[:64] + out[64:] + dot(high, right_low)
+            blocks.append(jnp.concatenate([out, pad], axis=1))
+        for t in range(4):
+            total = blocks[0][t * 16 : t * 16 + 8]
+            for part, member in ((0, 1), (1, 0), (1, 1)):
+                at = t * 16 + member * 8
+                total = total + pltpu.roll(
+                    blocks[part][at : at + 8], 64 * part + 32 * member, 1
+                )
+            sends[t, r * 8 : (r + 1) * 8, :] = total
+    factors = jnp.concatenate([in_rows, out_rows, jnp.zeros((16, 64), F32)], axis=1)
+    for t in range(4):
+        sends[t, 64:80, :] = factors
+
+
+def forward_kernel(
+    grid_ref, core_ref, ty_ref, tz_ref, y_ref, z_ref, x_ref, reach_ref, in_ref, out_factor_ref,
+    send_ref, s0, s1, s2, s3, scale_ref,
+    stage, core, ty, tz, y, z, x, reach, in_rows, out_rows, lines, send, sends, scale,
+    arrive, small, leave,
+):
     count = stage.shape[0]
     per_chunk = count // CHUNKS
+    gx = lax.axis_index("gx")
+    col = lax.axis_index("col")
 
     def chunk_copy(n):
         part = pl.ds(n * per_chunk, per_chunk)
         return pltpu.make_async_copy(grid_ref.at[part], stage.at[part], arrive.at[n])
 
+    pairs = (
+        (y_ref, y), (z_ref, z), (x_ref, x), (reach_ref, reach), (in_ref, in_rows),
+        (out_factor_ref, out_rows), (core_ref, core), (ty_ref, ty), (tz_ref, tz),
+    )
+    copies = [
+        pltpu.make_async_copy(source, target, small.at[n])
+        for n, (source, target) in enumerate(pairs)
+    ]
+    for copy in copies[:7]:
+        copy.start()
     for n in range(CHUNKS):
         chunk_copy(n).start()
-    table = ty_ref[...]
+        if n == 0:
+            for copy in copies[7:]:
+                copy.start()
+    for copy in copies[:6]:
+        copy.wait()
+    high, low = column_picks(y[...], z[...], gx, col)
+    kept_scale(x[...], reach[...], gx, col, scale)
+    copies[6].wait()
+    contract_core(core, high, low, in_rows[...], out_rows[...], sends)
+    leaving = [pltpu.make_async_copy(scale, scale_ref, leave.at[0])]
+    for t, target in enumerate((s0, s1, s2, s3)):
+        leaving.append(pltpu.make_async_copy(sends.at[t], target, leave.at[1 + t]))
+    for copy in leaving:
+        copy.start()
+    copies[7].wait()
+    copies[8].wait()
+    table = ty[...]
     for n in range(CHUNKS):
         chunk_copy(n).wait()
         for at in range(n * per_chunk, (n + 1) * per_chunk, 2):
@@ -155,32 +245,46 @@
             out = out[:ROWS] + out[ROWS:]
             lines[pl.ds(at, ROWS, stride=count), :] = out[:, :128]
             lines[pl.ds(at + 1, ROWS, stride=count), :] = out[:, 128:]
-    tz = tz_ref[...]
-    tz_high = tz[:64]
+    both_tz = tz[...]
+    tz_high = both_tz[:64]
     contract = (((1,), (1,)), ((), ()))
-    pieces = []
-    for p in range(9):
+
+    def piece(p):
         at = p * 128
         values = jnp.concatenate(
             [lines[at : at + 128, :], lines[FREQ_ROWS * count + at : FREQ_ROWS * count + at + 128, :]],
             axis=1,
         )
         high, low = split(values)
-        first = lax.dot_general(tz, high, contract, preferred_element_type=F32)
+        first = lax.dot_general(both_tz, high, contract, preferred_element_type=F32)
         second = lax.dot_general(tz_high, low, contract, preferred_element_type=F32)
-        pieces.append(first[:64] + first[64:] + second)
+        return first[:64] + first[64:] + second
+
+    def ship(n):
+        part = pl.ds(n * 128, 128)
+        copy = pltpu.make_async_copy(send.at[part], send_ref.at[part], leave.at[5 + n])
+        leaving.append(copy)
+        copy.start()
+
     lane = lax.broadcasted_iota(jnp.int32, (32, 128), 1)
-    for p in range(8):
-        send_ref[p * 32 : (p + 1) * 32, :] = pieces[p][:32]
-        if p > 0:
-            send_ref[256 + p * 32 : 256 + (p + 1) * 32, :] = pieces[p][32:]
-    send_ref[256:288, :] = jnp.where(lane < 64, pieces[8][32:], pieces[0][32:])
+    edges = piece(0), piece(8)
+    send[0:32, :] = edges[0][:32]
+    send[256:288, :] = jnp.where(lane < 64, edges[1][32:], edges[0][32:])
+    for p in range(1, 8):
+        values = piece(p)
+        send[p * 32 : (p + 1) * 32, :] = values[:32]
+        send[256 + p * 32 : 256 + (p + 1) * 32, :] = values[32:]
+        if p % 4 == 3:
+            ship(p // 4)
+            ship(2 + p // 4)
+    for copy in leaving:
+        copy.wait()
 
 
 def middle_kernel(
-    got_ref, tx_ref, sum_ref, win_ref, scale_ref, core_ref, wout_ref, spread_ref, vx_ref, send_ref
+    got_ref, tables_ref, win_ref, scale_ref, core_ref, wout_ref, send_ref
 ):
-    tx = tx_ref[...]
+    tx = table_of(tables_ref, "tx")
     lane = lax.broadcasted_iota(jnp.int32, (64, 128), 1)
     waves = []
     for pair in range(2):
@@ -194,7 +298,7 @@
                 picked = jnp.where(lane % 4 == x, part[x * 64 : (x + 1) * 64], picked)
             waves.append(picked)
     high, low = split(jnp.concatenate(waves, axis=1))
-    spectrum = dot(jnp.concatenate([high, low], axis=0), sum_ref[...])
+    spectrum = dot(jnp.concatenate([high, low], axis=0), table_of(tables_ref, "sum"))
     high, low = split(spectrum[:64] + spectrum[64:])
     amplitude = dot(jnp.concatenate([high, low, high], axis=1), win_ref[...])
     scale = scale_ref[...]
@@ -215,8 +319,8 @@
         preferred_element_type=F32,
     )
     high, low = split(spectra)
-    both = dot(jnp.concatenate([high, low], axis=0), spread_ref[...])
-    vx = vx_ref[...]
+    both = dot(jnp.concatenate([high, low], axis=0), table_of(tables_ref, "spread"))
+    vx = table_of(tables_ref, "vx")
     zero = jnp.zeros((64, 128), F32)
     for pair in range(2):
         sides = []
@@ -288,59 +392,8 @@
     return jnp.where(block < 8, 2 * block + member, tail)
 
 
-def core_kernel(
-    core_ref, y_ref, z_ref, in_ref, out_factor_ref, s0, s1, s2, s3
-):
-    gx = lax.axis_index("gx")
+def weights_kernel(p0, p1, p2, p3, tables_ref, win_ref, core_ref, wout_ref, tall):
     col = lax.axis_index("col")
-    row = lax.broadcasted_iota(jnp.int32, (8, 32), 0)
-    lane = lax.broadcasted_iota(jnp.int32, (8, 32), 1)
-    block = ((col + row // 2) % 4) * 4 + gx // 16
-    chosen_y = (slot_of(block, row % 2) == lane).astype(F32)
-    chosen_z = (lane[:, :16] == gx % 16).astype(F32)
-    y_rows = exact_dot(chosen_y, y_ref[...], (1, 1))
-    z_rows = exact_dot(chosen_z, z_ref[...], (1, 1))
-    pick = exact_dot(y_rows, repeater(8, 256, 4)) * exact_dot(z_rows, repeater(4, 256, 1))
-    tall = jnp.concatenate(
-        [jnp.broadcast_to(pick[n : n + 1], (8, 256)) for n in range(8)], axis=0
-    )
-    row = lax.broadcasted_iota(jnp.int32, (64, 256), 0)
-    lane = lax.broadcasted_iota(jnp.int32, (64, 256), 1)
-    tall = jnp.where(row % 8 == lane // 32, tall, 0.0)
-    high, low = split(tall)
-    both = jnp.concatenate([high, low], axis=0)
-    pad = jnp.zeros((64, 96), F32)
-    sends = (s0, s1, s2, s3)
-    for r in range(8):
-        blocks = []
-        for part in range(2):
-            at = (part * 8 + r) * 256
-            values = core_ref[at : at + 256, :]
-            right_high, right_low = split(values)
-            out = dot(both, right_high)
-            out = out[:64] + out[64:] + dot(high, right_low)
-            blocks.append(jnp.concatenate([out, pad], axis=1))
-        for t in range(4):
-            total = blocks[0][t * 16 : t * 16 + 8]
-            for part, member in ((0, 1), (1, 0), (1, 1)):
-                at = t * 16 + member * 8
-                total = total + pltpu.roll(
-                    blocks[part][at : at + 8], 64 * part + 32 * member, 1
-                )
-            sends[t][r * 8 : (r + 1) * 8, :] = total
-    factors = jnp.concatenate(
-        [in_ref[...], out_factor_ref[...], jnp.zeros((16, 64), F32)], axis=1
-    )
-    for t in range(4):
-        sends[t][64:80, :] = factors
-
-
-def weights_kernel(
-    p0, p1, p2, p3, x_ref, reach_ref, repeat_ref, win_ref, scale_ref, core_ref, wout_ref, tall
-):
-    gx = lax.axis_index("gx")
-    col = lax.axis_index("col")
-    kz = gx % 16
     for t, piece in enumerate((p0, p1, p2, p3)):
         source = (col - t + 4) % 4
         high, low = split(piece[:64, :])
@@ -350,7 +403,7 @@
         core_ref[pl.ds(pl.multiple_of(512 + at, 64), 64), :] = low
         tall[pl.ds(pl.multiple_of(source * 16, 16), 16), :] = piece[64:, :]
     high, low = split(tall[...])
-    spread = dot(jnp.concatenate([high, low], axis=0), repeat_ref[...])
+    spread = dot(jnp.concatenate([high, low], axis=0), table_of(tables_ref, "repeat"))
     zero = jnp.zeros((64, 256), F32)
     tops = []
     for values in (spread[:64, :256], spread[64:, :256]):
@@ -368,28 +421,20 @@
         for values in (spread[:64], spread[64:])
     ]
     wout_ref[...] = jnp.concatenate([outs[0], outs[0], outs[1]], axis=1)
-    slot = lax.broadcasted_iota(jnp.int32, (32, 256), 0)
-    freq = jnp.where(slot < 16, slot, 32 - slot)
-    weight = jnp.where(kz == 0, 1.0, 2.0).astype(F32)
-    block = col * 4 + gx // 16
-    wide = exact_dot(x_ref[...], repeater(8, 256, 1)) * weight
-    for member in range(2):
-        reach = reach_ref[kz, slot_of(block, member)]
-        scale_ref[:, member * 256 : (member + 1) * 256] = jnp.where(freq < reach, wide, 0.0)
-
-
-def inverse_kernel(got_ref, tz_ref, vy_ref, out_ref, lines, stage, leave):
+
+def inverse_kernel(got_ref, tables_ref, out_ref, lines, stage, leave):
     count = stage.shape[0]
     per_chunk = count // CHUNKS
     lines[2 * FREQ_ROWS * count :, :] = jnp.zeros(
         ((ROWS - 2 * FREQ_ROWS) * count, 128), F32
     )
+    tz = [table_of(tables_ref, "tz0"), table_of(tables_ref, "tz1")]
     row = lax.broadcasted_iota(jnp.int32, (128, 128), 0)
     lane = lax.broadcasted_iota(jnp.int32, (128, 128), 1)
 
     def emit(p, values, pick):
         high, low = split(values)
-        out = dot(jnp.concatenate([high, high, low], axis=1), tz_ref[pick])
+        out = dot(jnp.concatenate([high, high, low], axis=1), tz[pick])
         lines[p * 128 : (p + 1) * 128, :] = out[:, :128]
         at = FREQ_ROWS * count + p * 128
         lines[at : at + 128, :] = out[:, 128:]
@@ -411,7 +456,7 @@
         part = pl.ds(n * per_chunk, per_chunk)
         return pltpu.make_async_copy(stage.at[part], out_ref.at[part], leave.at[n])
 
-    vy = vy_ref[...]
+    vy = table_of(tables_ref, "vy")
     for n in range(CHUNKS):
         for at in range(n * per_chunk, (n + 1) * per_chunk, 2):
             both = jnp.concatenate(
@@ -433,87 +478,111 @@
         chunk_copy(n).wait()
 
 
+def parts_of_tables():
+    tz = z_inverse_table()
+    return {
+        "repeat": repeat_tables(),
+        "tx": x_forward_table(),
+        "sum": sum_table(),
+        "spread": spread_table(),
+        "vx": x_inverse_table(),
+        "tz0": tz[0],
+        "tz1": tz[1],
+        "vy": y_inverse_table(),
+    }
+
+
+@functools.cache
+def all_tables():
+    places, blocks, at = {}, [], 0
+    for name, table in parts_of_tables().items():
+        places[name] = (at, *table.shape)
+        for lane in range(0, table.shape[1], 128):
+            blocks.append(table[:, lane : lane + 128])
+            at += table.shape[0]
+    return places, np.concatenate(blocks, 0)
+
+
+def table_of(tables_ref, name):
+    at, rows, lanes = all_tables()[0][name]
+    return jnp.concatenate(
+        [tables_ref[at + n * rows : at + (n + 1) * rows, :] for n in range(lanes // 128)], axis=1
+    )
+
+
 VMEM = pl.BlockSpec(memory_space=pltpu.VMEM)
+HBM = pl.BlockSpec(memory_space=pltpu.HBM)
 
 
 def room(mebibytes):
     return pltpu.CompilerParams(vmem_limit_bytes=mebibytes << 20)
 
 
-HBM = pl.BlockSpec(memory_space=pltpu.HBM)
-
-
-def forward_call(grid_field):
+def forward_call(grid_field, core, y_factor, z_factor, x_factor, kx_reach, in_factor, out_factor):
     count, grid_y, grid_z = grid_field.shape
+    operands = (
+        grid_field, core, y_forward_table(), z_forward_table(), y_factor.T, z_factor.T,
+        x_factor.T, kx_reach.T, in_factor, out_factor,
+    )
+    piece = jax.ShapeDtypeStruct((80, 128), F32)
     return pl.pallas_call(
         forward_kernel,
-        out_shape=pltpu.VMEM((512, 128), F32),
-        in_specs=[HBM, VMEM, VMEM],
-        out_specs=VMEM,
-        scratch_shapes=[
-            pltpu.VMEM((count, grid_y, grid_z), BF16),
+        out_shape=(
+            jax.ShapeDtypeStruct((512, 128), F32),
+            piece,
+            piece,
+            piece,
+            piece,
+            jax.ShapeDtypeStruct((32, 512), F32),
+        ),
+        in_specs=[HBM] * len(operands),
+        out_specs=(HBM,) * 6,
+        scratch_shapes=[pltpu.VMEM(value.shape, value.dtype) for value in operands]
+        + [
             pltpu.VMEM((ROWS * count, 128), F32),
+            pltpu.VMEM((512, 128), F32),
+            pltpu.VMEM((4, 80, 128), F32),
+            pltpu.VMEM((32, 512), F32),
             pltpu.SemaphoreType.DMA((CHUNKS,)),
+            pltpu.SemaphoreType.DMA((9,)),
+            pltpu.SemaphoreType.DMA((9,)),
         ],
         name="forward_yz",
-    )(grid_field, y_forward_table(), z_forward_table())
+    )(*operands)
 
 
 def middle_call(got, win, scale, core, wout):
     return pl.pallas_call(
         middle_kernel,
-        out_shape=pltpu.VMEM((512, 128), F32),
-        in_specs=[VMEM] * 9,
+        out_shape=jax.ShapeDtypeStruct((512, 128), F32),
+        in_specs=[VMEM] * 6,
         out_specs=VMEM,
         compiler_params=room(12),
         name="mix_columns",
-    )(
-        got,
-        x_forward_table(),
-        sum_table(),
-        win,
-        scale,
-        core,
-        wout,
-        spread_table(),
-        x_inverse_table(),
-    )
-
-
-def core_call(core, y_factor, z_factor, in_factor, out_factor):
-    piece = pltpu.VMEM((80, 128), F32)
-    return pl.pallas_call(
-        core_kernel,
-        out_shape=(piece,) * 4,
-        in_specs=[VMEM] * 5,
-        out_specs=(VMEM,) * 4,
-        compiler_params=room(12),
-        name="contract_core",
-    )(core, y_factor.T, z_factor.T, in_factor, out_factor)
-
-
-def weights_call(pieces, x_factor, kx_reach):
+    )(got, all_tables()[1], win, scale, core, wout)
+
+
+def weights_call(pieces):
     return pl.pallas_call(
         weights_kernel,
         out_shape=(
-            pltpu.VMEM((384, 512), BF16),
-            pltpu.VMEM((32, 512), F32),
-            pltpu.VMEM((768, 128), BF16),
-            pltpu.VMEM((128, 384), BF16),
+            jax.ShapeDtypeStruct((384, 512), BF16),
+            jax.ShapeDtypeStruct((768, 128), BF16),
+            jax.ShapeDtypeStruct((128, 384), BF16),
         ),
-        in_specs=[VMEM] * 5 + [pl.BlockSpec(memory_space=pltpu.SMEM)] + [VMEM],
-        out_specs=(VMEM,) * 4,
+        in_specs=[VMEM] * 5,
+        out_specs=(VMEM,) * 3,
         scratch_shapes=[pltpu.VMEM((64, 128), F32)],
         compiler_params=room(12),
         name="build_weights",
-    )(*pieces, x_factor, kx_reach.T, repeat_tables())
+    )(*pieces, all_tables()[1])
 
 
 def inverse_call(got, count, grid_y, grid_z):
     return pl.pallas_call(
         inverse_kernel,
-        out_shape=pltpu.HBM((count, grid_y, grid_z), BF16),
-        in_specs=[VMEM] * 3,
+        out_shape=jax.ShapeDtypeStruct((count, grid_y, grid_z), BF16),
+        in_specs=[VMEM] * 2,
         out_specs=HBM,
         scratch_shapes=[
             pltpu.VMEM((ROWS * count, 128), F32),
@@ -522,7 +591,7 @@
         ],
         compiler_params=room(16),
         name="inverse_yz",
-    )(got, z_inverse_table(), y_inverse_table())
+    )(got, all_tables()[1])
 
 
 def swap_over_col(pieces):
@@ -544,11 +613,19 @@
 ):
     channels, planes, grid_y, grid_z = grid_field.shape
     count = channels * planes
-    sent = forward_call(grid_field.reshape(count, grid_y, grid_z))
+    core = jnp.transpose(tucker_core, (0, 1, 3, 4, 5, 2)).reshape(-1, tucker_core.shape[2])
+    sent, *pieces, scale = forward_call(
+        grid_field.reshape(count, grid_y, grid_z),
+        core,
+        y_factor,
+        z_factor,
+        x_factor,
+        kx_reach,
+        in_factor,
+        out_factor,
+    )
     got = everyone(sent)
-    core = jnp.transpose(tucker_core, (0, 1, 3, 4, 5, 2)).reshape(-1, tucker_core.shape[2])
-    pieces = core_call(core, y_factor, z_factor, in_factor, out_factor)
-    win, scale, core, wout = weights_call(swap_over_col(pieces), x_factor, kx_reach)
+    win, core, wout = weights_call(swap_over_col(pieces))
     sent = middle_call(got, win, scale, core, wout)
     got = everyone(sent)
     result = inverse_call(got, count, grid_y, grid_z)

time: 70.2 us -> 66.3 us (0.944)
  waiting for transfers between devices: 4.22 us -> 9.9 us
  blocking collectives: 27.6 us -> 22.6 us
  local copies, waits for them, and re-layouts: 5.09 us -> 1.62 us
  Pallas kernels: 12.3 us -> 11.2 us
    all_to_all x1, blocking collectives: 27.6 us -> 22.6 us  [everyone(): lax.all_to_all(values, ('col', 'gx'), 0, 0, tiled=True).reshape(512, 128)]
    all_to_all x1, waiting for transfers between devices: 2.6 us -> 7.4 us  [everyone(): lax.all_to_all(values, ('col', 'gx'), 0, 0, tiled=True).reshape(512, 128)]
    unnamed x31 -> x6, local copies, waits for them, and re-layouts: 5.09 us -> 1.62 us
    pallas_call x5 -> x4, Pallas kernels: 12.3 us -> 11.2 us  [the longest x1 6.74 us: forward_call(): pl.pallas_call(forward_kernel, out_shape=(jax.ShapeDtypeStruct((512, 128)...]
    ppermute x3, waiting for transfers between devices: 1.62 us -> 2.5 us  [swap_over_col(): arrived.append(lax.ppermute(pieces[step], 'col', ring))]
  transfers between devices with their start and end apart: 4 -> 4, of which waited for: 2 -> 3; matrix products, arithmetic and copies ran while one was open for 1% -> 0% of each run, Pallas kernels for 4% -> 0%
where the time goes in v3:
time: 66.3 us; the launch traced here: 66 us
  blocking collectives  22.6 us (34%)
  starting transfers between devices  20.7 us (31%)
  Pallas kernels  11.2 us (17%)
  waiting for transfers between devices  9.9 us (15%)
  local copies, waits for them, and re-layouts  1.62 us (2%)
    all_to_all x1, blocking collectives, everyone(): lax.all_to_all(values, ('col', 'gx'), 0, 0, tiled=True).reshape(512, 128)  22.6 us
    all_to_all x1, starting transfers between devices, everyone(): lax.all_to_all(values, ('col', 'gx'), 0, 0, tiled=True).reshape(512, 128)  15.7 us
    all_to_all x1, waiting for transfers between devices, everyone(): lax.all_to_all(values, ('col', 'gx'), 0, 0, tiled=True).reshape(512, 128)  7.4 us
    pallas_call x1, Pallas kernels, forward_call(): pl.pallas_call(forward_kernel, out_shape=(jax.ShapeDtypeStruct((512, 128)...  6.74 us
    ppermute x3, starting transfers between devices, swap_over_col(): arrived.append(lax.ppermute(pieces[step], 'col', ring))  5.01 us
    pallas_call x1, Pallas kernels, inverse_call(): pl.pallas_call(inverse_kernel, out_shape=jax.ShapeDtypeStruct((count, gri...  2.93 us
    ppermute x3, waiting for transfers between devices, swap_over_col(): arrived.append(lax.ppermute(pieces[step], 'col', ring))  2.5 us
    unnamed x6, local copies, waits for them, and re-layouts  1.62 us
  transfers between devices with their start and end apart: 4, of which 3 were waited for; matrix products, arithmetic and copies ran while one was open for 0% of the time, Pallas kernels for 0%

profile of v3, /device:TPU:1, one launch (start us, length us, event | category | flops | bytes accessed | tf_op | source)
XLA Modules:
  0.0 66.0 jit_solution(3673197844175243046)
XLA Ops:
  0.0 0.0 copy-start
  0.0 6.7 %forward_yz.1 = (f32[512,128]{1,0:T(8,128)}, f32[80,128]{1,0:T(8,128)}, f32[80,128]{1,0:T(8,128)}, f32[80,128]{1,0:T(8,128)}, f32[80,128]{1,0:T(8,128)}, /*index=5*/f32[32,512]{1,0:T(8,128)}) custom-call(bf16[64,256,128]{2,1,0:T(8,128)(2,1)} %bitcast.16, f32[4096,32]{1,0:T(8,128)} %bitcast.17, bf16[80,256]{1,0:T(8,128)(2,1)} %constant.6.clone.ty_ref, ...), custom_call_target="tpu_custom_call" | custom-call | tf_op jit(solution)/shard_map/forward_yz/pallas_call | solution.py:528
  6.8 15.7 %all-to-all-start = ((f32[256,2,128]{2,1,0:T(2,128)}), f32[256,2,128]{2,1,0:T(2,128)S(1)}, u32[]{:S(2)}, u32[]{:S(2)}) async-start(f32[256,2,128]{2,1,0:T(2,128)} %bitcast.18), calls=%async_computation | async-start | bytes 524288 | tf_op jit(solution)/shard_map/all_to_all | solution.py:608
  22.4 1.4 %collective-permute-start = (f32[80,128]{1,0:T(8,128)}, f32[80,128]{1,0:T(8,128)S(1)}, u32[]{:S(2)}, u32[]{:S(2)}) collective-permute-start(f32[80,128]{1,0:T(8,128)} %get-tuple-element.16), channel_id=1, source_target_pairs={{0,1},{1,2},{2,3},{3,0},{4,5},{5,6},{6,7},{7,4},{8,9},{9,10},{10,1... | collective-permute-start | bytes 122888 | tf_op jit(solution)/shard_map/ppermute | solution.py:602
  23.8 2.5 %collective-permute-start.1 = (f32[80,128]{1,0:T(8,128)}, f32[80,128]{1,0:T(8,128)S(1)}, u32[]{:S(2)}, u32[]{:S(2)}) collective-permute-start(f32[80,128]{1,0:T(8,128)} %get-tuple-element.17), channel_id=1, source_target_pairs={{0,2},{1,3},{2,0},{3,1},{4,6},{5,7},{6,4},{7,5},{8,10},{9,11},{10,... | collective-permute-start | bytes 122888 | tf_op jit(solution)/shard_map/ppermute | solution.py:602
  26.3 1.1 %collective-permute-start.2 = (f32[80,128]{1,0:T(8,128)}, f32[80,128]{1,0:T(8,128)S(1)}, u32[]{:S(2)}, u32[]{:S(2)}) collective-permute-start(f32[80,128]{1,0:T(8,128)} %get-tuple-element.18), channel_id=1, source_target_pairs={{0,3},{1,0},{2,1},{3,2},{4,7},{5,4},{6,5},{7,6},{8,11},{9,8},{10,9... | collective-permute-start | bytes 122888 | tf_op jit(solution)/shard_map/ppermute | solution.py:602
  27.4 0.0 collective-permute-done.p1
  27.4 1.7 %collective-permute-done.1.p2 = f32[80,128]{1,0:T(8,128)S(1)} collective-permute-done((f32[80,128]{1,0:T(8,128)}, f32[80,128]{1,0:T(8,128)S(1)}, u32[]{:S(2)}, u32[]{:S(2)}) %collective-permute-start.1) | collective-permute-done | bytes 40992 | tf_op jit(solution)/shard_map/ppermute | solution.py:602
  29.1 0.8 %collective-permute-done.2.p3 = f32[80,128]{1,0:T(8,128)S(1)} collective-permute-done((f32[80,128]{1,0:T(8,128)}, f32[80,128]{1,0:T(8,128)S(1)}, u32[]{:S(2)}, u32[]{:S(2)}) %collective-permute-start.2) | collective-permute-done | bytes 40992 | tf_op jit(solution)/shard_map/ppermute | solution.py:602
  29.9 0.0 copy-done
  29.9 0.0 copy-start.2
  29.9 0.8 %copy-done.2 = f32[80,128]{1,0:T(8,128)S(1)} copy-done((f32[80,128]{1,0:T(8,128)S(1)}, f32[80,128]{1,0:T(8,128)}, u32[]{:S(2)}) %copy-start.2) | copy-done | bytes 40984
  30.7 0.2 build_weights.1
  30.9 7.4 %all-to-all-done = f32[256,2,128]{2,1,0:T(2,128)S(1)} async-done(((f32[256,2,128]{2,1,0:T(2,128)}), f32[256,2,128]{2,1,0:T(2,128)S(1)}, u32[]{:S(2)}, u32[]{:S(2)}) %all-to-all-start) | async-done | bytes 262176 | tf_op jit(solution)/shard_map/all_to_all | solution.py:608
  38.3 0.0 copy-start.1
  38.3 0.8 %copy-done.1 = f32[32,512]{1,0:T(8,128)S(1)} copy-done((f32[32,512]{1,0:T(8,128)S(1)}, f32[32,512]{1,0:T(8,128)}, u32[]{:S(2)}) %copy-start.1) | copy-done | bytes 65560
  39.2 1.3 %mix_columns.1 = f32[512,128]{1,0:T(8,128)S(1)} custom-call(f32[512,128]{1,0:T(8,128)S(1)} %bitcast.13, bf16[4864,128]{1,0:T(8,128)(2,1)S(1)} %copy-done, bf16[384,512]{1,0:T(8,128)(2,1)S(1)} %get-tuple-element.19.win_ref, f32[32,512]{1,0:T(8,128)S(1)} %copy-done.1, bf16[768,128]{1,0:T(8,128)(2,1)S(1)} %get-tuple-element.21.core_ref, ...), custom_call_target="tpu_custom_call" | custom-call | tf_op jit(solution)/shard_map/mix_columns/pallas_call | solution.py:555
  40.5 22.6 %all_to_all.10 = f32[256,2,128]{2,1,0:T(2,128)S(1)} all-to-all(f32[256,2,128]{2,1,0:T(2,128)S(1)} %bitcast.14), channel_id=1, replica_groups=mesh['gx'=64,'col'=4] {'col','gx'}, dimensions={0} | all-to-all | bytes 524288 | tf_op jit(solution)/shard_map/all_to_all | solution.py:608
  63.1 2.9 %inverse_yz.1 = bf16[64,256,128]{2,1,0:T(8,128)(2,1)} custom-call(f32[512,128]{1,0:T(8,128)S(1)} %bitcast.15, bf16[4864,128]{1,0:T(8,128)(2,1)S(1)} %copy-done), custom_call_target="tpu_custom_call" | custom-call | tf_op jit(solution)/shard_map/inverse_yz/pallas_call | solution.py:582
Async XLA Ops:
  0.0 29.9 %copy-start = (bf16[4864,128]{1,0:T(8,128)(2,1)S(1)}, bf16[4864,128]{1,0:T(8,128)(2,1)}, u32[]{:S(2)}) copy-start(bf16[4864,128]{1,0:T(8,128)(2,1)} %constant.8.clone.tables_ref) | copy-start | bytes 3735556
  6.8 31.6 %all-to-all-start = ((f32[256,2,128]{2,1,0:T(2,128)}), f32[256,2,128]{2,1,0:T(2,128)S(1)}, u32[]{:S(2)}, u32[]{:S(2)}) async-start(f32[256,2,128]{2,1,0:T(2,128)} %bitcast.18), calls=%async_computation | async-start | bytes 524288 | tf_op jit(solution)/shard_map/all_to_all | solution.py:608
  22.4 5.0 %collective-permute-start = (f32[80,128]{1,0:T(8,128)}, f32[80,128]{1,0:T(8,128)S(1)}, u32[]{:S(2)}, u32[]{:S(2)}) collective-permute-start(f32[80,128]{1,0:T(8,128)} %get-tuple-element.16), channel_id=1, source_target_pairs={{0,1},{1,2},{2,3},{3,0},{4,5},{5,6},{6,7},{7,4},{8,9},{9,10},{10,1... | collective-permute-start | bytes 122888 | tf_op jit(solution)/shard_map/ppermute | solution.py:602
  23.8 5.3 %collective-permute-start.1 = (f32[80,128]{1,0:T(8,128)}, f32[80,128]{1,0:T(8,128)S(1)}, u32[]{:S(2)}, u32[]{:S(2)}) collective-permute-start(f32[80,128]{1,0:T(8,128)} %get-tuple-element.17), channel_id=1, source_target_pairs={{0,2},{1,3},{2,0},{3,1},{4,6},{5,7},{6,4},{7,5},{8,10},{9,11},{10,... | collective-permute-start | bytes 122888 | tf_op jit(solution)/shard_map/ppermute | solution.py:602
  26.3 3.6 %collective-permute-start.2 = (f32[80,128]{1,0:T(8,128)}, f32[80,128]{1,0:T(8,128)S(1)}, u32[]{:S(2)}, u32[]{:S(2)}) collective-permute-start(f32[80,128]{1,0:T(8,128)} %get-tuple-element.18), channel_id=1, source_target_pairs={{0,3},{1,0},{2,1},{3,2},{4,7},{5,4},{6,5},{7,6},{8,11},{9,8},{10,9... | collective-permute-start | bytes 122888 | tf_op jit(solution)/shard_map/ppermute | solution.py:602
  29.9 0.8 %copy-start.2 = (f32[80,128]{1,0:T(8,128)S(1)}, f32[80,128]{1,0:T(8,128)}, u32[]{:S(2)}) copy-start(f32[80,128]{1,0:T(8,128)} %get-tuple-element.15.p0) | copy-start | bytes 122884
  38.3 0.8 %copy-start.1 = (f32[32,512]{1,0:T(8,128)S(1)}, f32[32,512]{1,0:T(8,128)}, u32[]{:S(2)}) copy-start(f32[32,512]{1,0:T(8,128)} %get-tuple-element.20.scale_ref) | copy-start | bytes 196612

commit v4 on v3

--- a/solution.py
+++ b/solution.py
@@ -14,6 +14,7 @@
 BF16 = jnp.bfloat16
 FREQ_ROWS = 18
 ROWS = 40
+PITCH = 68
 
 
 def halves(table):
@@ -133,7 +134,8 @@
     return np.concatenate([high, low, high], 1)
 
 
-CHUNKS = 8
+IN_CHUNKS = 4
+OUT_CHUNKS = 8
 
 
 def column_picks(y, z, gx, col):
@@ -166,7 +168,9 @@
         here = (row == kz) & (lane == slot_of(block, member))
         bound = jnp.sum(jnp.where(here, reach.astype(F32), 0.0), axis=1, keepdims=True)
         bound = jnp.sum(bound, axis=0, keepdims=True)
-        scale_ref[:, member * 256 : (member + 1) * 256] = jnp.where(freq < bound, wide, 0.0)
+        kept = jnp.where(freq < bound, wide, 0.0)
+        scale_ref[member * 64 : member * 64 + 32, :] = kept[:, :128]
+        scale_ref[member * 64 + 32 : member * 64 + 64, :] = kept[:, 128:]
 
 
 def contract_core(core, high, low, in_rows, out_rows, sends):
@@ -195,12 +199,12 @@
 
 def forward_kernel(
     grid_ref, core_ref, ty_ref, tz_ref, y_ref, z_ref, x_ref, reach_ref, in_ref, out_factor_ref,
-    send_ref, s0, s1, s2, s3, scale_ref,
+    send_ref, s0, s1, s2, s3,
     stage, core, ty, tz, y, z, x, reach, in_rows, out_rows, lines, send, sends, scale,
     arrive, small, leave,
 ):
     count = stage.shape[0]
-    per_chunk = count // CHUNKS
+    per_chunk = count // IN_CHUNKS
     gx = lax.axis_index("gx")
     col = lax.axis_index("col")
 
@@ -216,43 +220,42 @@
         pltpu.make_async_copy(source, target, small.at[n])
         for n, (source, target) in enumerate(pairs)
     ]
-    for copy in copies[:7]:
+    for copy in copies[:6]:
         copy.start()
-    for n in range(CHUNKS):
+    chunk_copy(0).start()
+    for copy in copies[7:]:
+        copy.start()
+    for n in range(1, IN_CHUNKS):
         chunk_copy(n).start()
-        if n == 0:
-            for copy in copies[7:]:
-                copy.start()
+    copies[6].start()
+    leaving = []
     for copy in copies[:6]:
         copy.wait()
     high, low = column_picks(y[...], z[...], gx, col)
     kept_scale(x[...], reach[...], gx, col, scale)
-    copies[6].wait()
-    contract_core(core, high, low, in_rows[...], out_rows[...], sends)
-    leaving = [pltpu.make_async_copy(scale, scale_ref, leave.at[0])]
-    for t, target in enumerate((s0, s1, s2, s3)):
-        leaving.append(pltpu.make_async_copy(sends.at[t], target, leave.at[1 + t]))
-    for copy in leaving:
-        copy.start()
     copies[7].wait()
     copies[8].wait()
     table = ty[...]
-    for n in range(CHUNKS):
+    for n in range(IN_CHUNKS):
         chunk_copy(n).wait()
         for at in range(n * per_chunk, (n + 1) * per_chunk, 2):
             both = jnp.concatenate([stage[at], stage[at + 1]], axis=1)
             out = dot(table, both)
             out = out[:ROWS] + out[ROWS:]
-            lines[pl.ds(at, ROWS, stride=count), :] = out[:, :128]
-            lines[pl.ds(at + 1, ROWS, stride=count), :] = out[:, 128:]
+            lines[pl.ds(at, ROWS, stride=PITCH), :] = out[:, :128]
+            lines[pl.ds(at + 1, ROWS, stride=PITCH), :] = out[:, 128:]
     both_tz = tz[...]
     tz_high = both_tz[:64]
     contract = (((1,), (1,)), ((), ()))
 
     def piece(p):
-        at = p * 128
         values = jnp.concatenate(
-            [lines[at : at + 128, :], lines[FREQ_ROWS * count + at : FREQ_ROWS * count + at + 128, :]],
+            [
+                jnp.concatenate(
+                    [lines[(at + n) * PITCH : (at + n) * PITCH + count, :] for n in range(2)], axis=0
+                )
+                for at in (2 * p, FREQ_ROWS + 2 * p)
+            ],
             axis=1,
         )
         high, low = split(values)
@@ -277,7 +280,14 @@
         if p % 4 == 3:
             ship(p // 4)
             ship(2 + p // 4)
-    for copy in leaving:
+    copies[6].wait()
+    contract_core(core, high, low, in_rows[...], out_rows[...], sends)
+    last = [pltpu.make_async_copy(scale, s0.at[pl.ds(80, 128)], leave.at[0])]
+    for t, target in enumerate((s0.at[pl.ds(0, 80)], s1, s2, s3)):
+        last.append(pltpu.make_async_copy(sends.at[t], target, leave.at[1 + t]))
+    for copy in last:
+        copy.start()
+    for copy in leaving + last:
         copy.wait()
 
 
@@ -392,8 +402,12 @@
     return jnp.where(block < 8, 2 * block + member, tail)
 
 
-def weights_kernel(p0, p1, p2, p3, tables_ref, win_ref, core_ref, wout_ref, tall):
+def weights_kernel(
+    p0, p1, p2, p3, tables_ref, win_ref, scale_ref, core_ref, wout_ref, tall
+):
     col = lax.axis_index("col")
+    for n in range(4):
+        scale_ref[:, n * 128 : (n + 1) * 128] = p0[80 + n * 32 : 112 + n * 32, :]
     for t, piece in enumerate((p0, p1, p2, p3)):
         source = (col - t + 4) % 4
         high, low = split(piece[:64, :])
@@ -401,7 +415,7 @@
         core_ref[pl.ds(pl.multiple_of(at, 64), 64), :] = high
         core_ref[pl.ds(pl.multiple_of(256 + at, 64), 64), :] = high
         core_ref[pl.ds(pl.multiple_of(512 + at, 64), 64), :] = low
-        tall[pl.ds(pl.multiple_of(source * 16, 16), 16), :] = piece[64:, :]
+        tall[pl.ds(pl.multiple_of(source * 16, 16), 16), :] = piece[64:80, :]
     high, low = split(tall[...])
     spread = dot(jnp.concatenate([high, low], axis=0), table_of(tables_ref, "repeat"))
     zero = jnp.zeros((64, 256), F32)
@@ -424,10 +438,9 @@
 
 def inverse_kernel(got_ref, tables_ref, out_ref, lines, stage, leave):
     count = stage.shape[0]
-    per_chunk = count // CHUNKS
-    lines[2 * FREQ_ROWS * count :, :] = jnp.zeros(
-        ((ROWS - 2 * FREQ_ROWS) * count, 128), F32
-    )
+    per_chunk = count // OUT_CHUNKS
+    for n in range(2 * FREQ_ROWS, ROWS):
+        lines[n * PITCH : n * PITCH + count, :] = jnp.zeros((count, 128), F32)
     tz = [table_of(tables_ref, "tz0"), table_of(tables_ref, "tz1")]
     row = lax.broadcasted_iota(jnp.int32, (128, 128), 0)
     lane = lax.broadcasted_iota(jnp.int32, (128, 128), 1)
@@ -435,9 +448,11 @@
     def emit(p, values, pick):
         high, low = split(values)
         out = dot(jnp.concatenate([high, high, low], axis=1), tz[pick])
-        lines[p * 128 : (p + 1) * 128, :] = out[:, :128]
-        at = FREQ_ROWS * count + p * 128
-        lines[at : at + 128, :] = out[:, 128:]
+        for n in range(2):
+            rows = out[n * count : (n + 1) * count]
+            for first, values in ((2 * p, rows[:, :128]), (FREQ_ROWS + 2 * p, rows[:, 128:])):
+                at = (first + n) * PITCH
+                lines[at : at + count, :] = values
 
     for t in range(4):
         block = jnp.concatenate(
@@ -457,12 +472,12 @@
         return pltpu.make_async_copy(stage.at[part], out_ref.at[part], leave.at[n])
 
     vy = table_of(tables_ref, "vy")
-    for n in range(CHUNKS):
+    for n in range(OUT_CHUNKS):
         for at in range(n * per_chunk, (n + 1) * per_chunk, 2):
             both = jnp.concatenate(
                 [
-                    lines[pl.ds(at, ROWS, stride=count), :],
-                    lines[pl.ds(at + 1, ROWS, stride=count), :],
+                    lines[pl.ds(at, ROWS, stride=PITCH), :],
+                    lines[pl.ds(at + 1, ROWS, stride=PITCH), :],
                 ],
                 axis=1,
             )
@@ -474,7 +489,7 @@
             stage[at] = out[:, :128]
             stage[at + 1] = out[:, 128:]
         chunk_copy(n).start()
-    for n in range(CHUNKS):
+    for n in range(OUT_CHUNKS):
         chunk_copy(n).wait()
 
 
@@ -529,21 +544,20 @@
         forward_kernel,
         out_shape=(
             jax.ShapeDtypeStruct((512, 128), F32),
+            jax.ShapeDtypeStruct((208, 128), F32),
             piece,
             piece,
             piece,
-            piece,
-            jax.ShapeDtypeStruct((32, 512), F32),
         ),
         in_specs=[HBM] * len(operands),
-        out_specs=(HBM,) * 6,
+        out_specs=(HBM,) * 5,
         scratch_shapes=[pltpu.VMEM(value.shape, value.dtype) for value in operands]
         + [
-            pltpu.VMEM((ROWS * count, 128), F32),
+            pltpu.VMEM((ROWS * PITCH, 128), F32),
             pltpu.VMEM((512, 128), F32),
             pltpu.VMEM((4, 80, 128), F32),
-            pltpu.VMEM((32, 512), F32),
-            pltpu.SemaphoreType.DMA((CHUNKS,)),
+            pltpu.VMEM((128, 128), F32),
+            pltpu.SemaphoreType.DMA((IN_CHUNKS,)),
             pltpu.SemaphoreType.DMA((9,)),
             pltpu.SemaphoreType.DMA((9,)),
         ],
@@ -567,11 +581,12 @@
         weights_kernel,
         out_shape=(
             jax.ShapeDtypeStruct((384, 512), BF16),
+            jax.ShapeDtypeStruct((32, 512), F32),
             jax.ShapeDtypeStruct((768, 128), BF16),
             jax.ShapeDtypeStruct((128, 384), BF16),
         ),
         in_specs=[VMEM] * 5,
-        out_specs=(VMEM,) * 3,
+        out_specs=(VMEM,) * 4,
         scratch_shapes=[pltpu.VMEM((64, 128), F32)],
         compiler_params=room(12),
         name="build_weights",
@@ -585,9 +600,9 @@
         in_specs=[VMEM] * 2,
         out_specs=HBM,
         scratch_shapes=[
-            pltpu.VMEM((ROWS * count, 128), F32),
+            pltpu.VMEM((ROWS * PITCH, 128), F32),
             pltpu.VMEM((count, grid_y, grid_z), BF16),
-            pltpu.SemaphoreType.DMA((CHUNKS,)),
+            pltpu.SemaphoreType.DMA((OUT_CHUNKS,)),
         ],
         compiler_params=room(16),
         name="inverse_yz",
@@ -614,7 +629,7 @@
     channels, planes, grid_y, grid_z = grid_field.shape
     count = channels * planes
     core = jnp.transpose(tucker_core, (0, 1, 3, 4, 5, 2)).reshape(-1, tucker_core.shape[2])
-    sent, *pieces, scale = forward_call(
+    sent, *pieces = forward_call(
         grid_field.reshape(count, grid_y, grid_z),
         core,
         y_factor,
@@ -625,7 +640,7 @@
         out_factor,
     )
     got = everyone(sent)
-    win, core, wout = weights_call(swap_over_col(pieces))
+    win, scale, core, wout = weights_call(swap_over_col(pieces))
     sent = middle_call(got, win, scale, core, wout)
     got = everyone(sent)
     result = inverse_call(got, count, grid_y, grid_z)

time: 66.3 us -> 63.6 us (0.959)
  Pallas kernels: 11.2 us -> 9.33 us
  local copies, waits for them, and re-layouts: 1.62 us -> 0.9 us
    pallas_call x1, Pallas kernels: 6.74 us -> 4.98 us  [forward_call(): pl.pallas_call(forward_kernel, out_shape=(jax.ShapeDtypeStruct((512, 128)...]
    unnamed x6 -> x4, local copies, waits for them, and re-layouts: 1.62 us -> 0.9 us
where the time goes in v4:
time: 63.6 us; the launch traced here: 63.5 us
  blocking collectives  22.8 us (36%)
  starting transfers between devices  20.7 us (33%)
  waiting for transfers between devices  9.78 us (15%)
  Pallas kernels  9.33 us (15%)
  local copies, waits for them, and re-layouts  0.9 us (1%)
    all_to_all x1, blocking collectives, everyone(): lax.all_to_all(values, ('col', 'gx'), 0, 0, tiled=True).reshape(512, 128)  22.8 us
    all_to_all x1, starting transfers between devices, everyone(): lax.all_to_all(values, ('col', 'gx'), 0, 0, tiled=True).reshape(512, 128)  15.7 us
    all_to_all x1, waiting for transfers between devices, everyone(): lax.all_to_all(values, ('col', 'gx'), 0, 0, tiled=True).reshape(512, 128)  7.28 us
    ppermute x3, starting transfers between devices, swap_over_col(): arrived.append(lax.ppermute(pieces[step], 'col', ring))  5.01 us
    pallas_call x1, Pallas kernels, forward_call(): pl.pallas_call(forward_kernel, out_shape=(jax.ShapeDtypeStruct((512, 128)...  4.98 us
    pallas_call x1, Pallas kernels, inverse_call(): pl.pallas_call(inverse_kernel, out_shape=jax.ShapeDtypeStruct((count, gri...  2.86 us
    ppermute x3, waiting for transfers between devices, swap_over_col(): arrived.append(lax.ppermute(pieces[step], 'col', ring))  2.5 us
    pallas_call x1, Pallas kernels, middle_call(): pl.pallas_call(middle_kernel, out_shape=jax.ShapeDtypeStruct((512, 128),...  1.3 us
  transfers between devices with their start and end apart: 4, of which 3 were waited for; matrix products, arithmetic and copies ran while one was open for 0% of the time, Pallas kernels for 0%

profile of v4, /device:TPU:1, one launch (start us, length us, event | category | flops | bytes accessed | tf_op | source)
XLA Modules:
  0.0 63.5 jit_solution(6895714750994096629)
XLA Ops:
  0.0 0.0 copy-start
  0.0 5.0 %forward_yz.1 = (f32[512,128]{1,0:T(8,128)}, f32[208,128]{1,0:T(8,128)}, f32[80,128]{1,0:T(8,128)}, f32[80,128]{1,0:T(8,128)}, f32[80,128]{1,0:T(8,128)}) custom-call(bf16[64,256,128]{2,1,0:T(8,128)(2,1)} %bitcast.16, f32[4096,32]{1,0:T(8,128)} %bitcast.17, bf16[80,256]{1,0:T(8,128)(2,1)} %constant.6.clone.ty_ref, bf16[128,256]{1,0:T(8,128)(2,1)} %constant.7.clone.tz_ref, ...), custom_call_target="tpu_custom_call" | custom-call | tf_op jit(solution)/shard_map/forward_yz/pallas_call | solution.py:543
  5.0 15.7 %all-to-all-start = ((f32[256,2,128]{2,1,0:T(2,128)}), f32[256,2,128]{2,1,0:T(2,128)S(1)}, u32[]{:S(2)}, u32[]{:S(2)}) async-start(f32[256,2,128]{2,1,0:T(2,128)} %bitcast.18), calls=%async_computation | async-start | bytes 524288 | tf_op jit(solution)/shard_map/all_to_all | solution.py:623
  20.7 1.4 %collective-permute-start = (f32[80,128]{1,0:T(8,128)}, f32[80,128]{1,0:T(8,128)S(1)}, u32[]{:S(2)}, u32[]{:S(2)}) collective-permute-start(f32[80,128]{1,0:T(8,128)} %get-tuple-element.16), channel_id=1, source_target_pairs={{0,1},{1,2},{2,3},{3,0},{4,5},{5,6},{6,7},{7,4},{8,9},{9,10},{10,1... | collective-permute-start | bytes 122888 | tf_op jit(solution)/shard_map/ppermute | solution.py:617
  22.1 2.5 %collective-permute-start.1 = (f32[80,128]{1,0:T(8,128)}, f32[80,128]{1,0:T(8,128)S(1)}, u32[]{:S(2)}, u32[]{:S(2)}) collective-permute-start(f32[80,128]{1,0:T(8,128)} %get-tuple-element.17), channel_id=1, source_target_pairs={{0,2},{1,3},{2,0},{3,1},{4,6},{5,7},{6,4},{7,5},{8,10},{9,11},{10,... | collective-permute-start | bytes 122888 | tf_op jit(solution)/shard_map/ppermute | solution.py:617
  24.5 1.1 %collective-permute-start.2 = (f32[80,128]{1,0:T(8,128)}, f32[80,128]{1,0:T(8,128)S(1)}, u32[]{:S(2)}, u32[]{:S(2)}) collective-permute-start(f32[80,128]{1,0:T(8,128)} %get-tuple-element.18), channel_id=1, source_target_pairs={{0,3},{1,0},{2,1},{3,2},{4,7},{5,4},{6,5},{7,6},{8,11},{9,8},{10,9... | collective-permute-start | bytes 122888 | tf_op jit(solution)/shard_map/ppermute | solution.py:617
  25.7 0.0 collective-permute-done.p1
  25.7 1.7 %collective-permute-done.1.p2 = f32[80,128]{1,0:T(8,128)S(1)} collective-permute-done((f32[80,128]{1,0:T(8,128)}, f32[80,128]{1,0:T(8,128)S(1)}, u32[]{:S(2)}, u32[]{:S(2)}) %collective-permute-start.1) | collective-permute-done | bytes 40992 | tf_op jit(solution)/shard_map/ppermute | solution.py:617
  27.4 0.8 %collective-permute-done.2.p3 = f32[80,128]{1,0:T(8,128)S(1)} collective-permute-done((f32[80,128]{1,0:T(8,128)}, f32[80,128]{1,0:T(8,128)S(1)}, u32[]{:S(2)}, u32[]{:S(2)}) %collective-permute-start.2) | collective-permute-done | bytes 40992 | tf_op jit(solution)/shard_map/ppermute | solution.py:617
  28.2 0.0 copy-done
  28.2 0.0 copy-start.1
  28.2 0.9 %copy-done.1 = f32[208,128]{1,0:T(8,128)S(1)} copy-done((f32[208,128]{1,0:T(8,128)S(1)}, f32[208,128]{1,0:T(8,128)}, u32[]{:S(2)}) %copy-start.1) | copy-done | bytes 106520
  29.1 0.2 build_weights.1
  29.3 7.3 %all-to-all-done = f32[256,2,128]{2,1,0:T(2,128)S(1)} async-done(((f32[256,2,128]{2,1,0:T(2,128)}), f32[256,2,128]{2,1,0:T(2,128)S(1)}, u32[]{:S(2)}, u32[]{:S(2)}) %all-to-all-start) | async-done | bytes 262176 | tf_op jit(solution)/shard_map/all_to_all | solution.py:623
  36.6 1.3 %mix_columns.1 = f32[512,128]{1,0:T(8,128)S(1)} custom-call(f32[512,128]{1,0:T(8,128)S(1)} %bitcast.13, bf16[4864,128]{1,0:T(8,128)(2,1)S(1)} %copy-done, bf16[384,512]{1,0:T(8,128)(2,1)S(1)} %get-tuple-element.19.win_ref, f32[32,512]{1,0:T(8,128)S(1)} %get-tuple-element.20.scale_ref, bf16[768,128]{1,0:T(8,128)(2,1)S(1)} %get-tuple-element.21.core_ref, ...), custom_call_target="tpu_custom_call" | custom-call | tf_op jit(solution)/shard_map/mix_columns/pallas_call | solution.py:569
  37.9 22.8 %all_to_all.10 = f32[256,2,128]{2,1,0:T(2,128)S(1)} all-to-all(f32[256,2,128]{2,1,0:T(2,128)S(1)} %bitcast.14), channel_id=1, replica_groups=mesh['gx'=64,'col'=4] {'col','gx'}, dimensions={0} | all-to-all | bytes 524288 | tf_op jit(solution)/shard_map/all_to_all | solution.py:623
  60.6 2.9 %inverse_yz.1 = bf16[64,256,128]{2,1,0:T(8,128)(2,1)} custom-call(f32[512,128]{1,0:T(8,128)S(1)} %bitcast.15, bf16[4864,128]{1,0:T(8,128)(2,1)S(1)} %copy-done), custom_call_target="tpu_custom_call" | custom-call | tf_op jit(solution)/shard_map/inverse_yz/pallas_call | solution.py:597
Async XLA Ops:
  0.0 28.2 %copy-start = (bf16[4864,128]{1,0:T(8,128)(2,1)S(1)}, bf16[4864,128]{1,0:T(8,128)(2,1)}, u32[]{:S(2)}) copy-start(bf16[4864,128]{1,0:T(8,128)(2,1)} %constant.8.clone.tables_ref) | copy-start | bytes 3735556
  5.0 31.6 %all-to-all-start = ((f32[256,2,128]{2,1,0:T(2,128)}), f32[256,2,128]{2,1,0:T(2,128)S(1)}, u32[]{:S(2)}, u32[]{:S(2)}) async-start(f32[256,2,128]{2,1,0:T(2,128)} %bitcast.18), calls=%async_computation | async-start | bytes 524288 | tf_op jit(solution)/shard_map/all_to_all | solution.py:623
  20.7 5.0 %collective-permute-start = (f32[80,128]{1,0:T(8,128)}, f32[80,128]{1,0:T(8,128)S(1)}, u32[]{:S(2)}, u32[]{:S(2)}) collective-permute-start(f32[80,128]{1,0:T(8,128)} %get-tuple-element.16), channel_id=1, source_target_pairs={{0,1},{1,2},{2,3},{3,0},{4,5},{5,6},{6,7},{7,4},{8,9},{9,10},{10,1... | collective-permute-start | bytes 122888 | tf_op jit(solution)/shard_map/ppermute | solution.py:617
  22.1 5.3 %collective-permute-start.1 = (f32[80,128]{1,0:T(8,128)}, f32[80,128]{1,0:T(8,128)S(1)}, u32[]{:S(2)}, u32[]{:S(2)}) collective-permute-start(f32[80,128]{1,0:T(8,128)} %get-tuple-element.17), channel_id=1, source_target_pairs={{0,2},{1,3},{2,0},{3,1},{4,6},{5,7},{6,4},{7,5},{8,10},{9,11},{10,... | collective-permute-start | bytes 122888 | tf_op jit(solution)/shard_map/ppermute | solution.py:617
  24.5 3.6 %collective-permute-start.2 = (f32[80,128]{1,0:T(8,128)}, f32[80,128]{1,0:T(8,128)S(1)}, u32[]{:S(2)}, u32[]{:S(2)}) collective-permute-start(f32[80,128]{1,0:T(8,128)} %get-tuple-element.18), channel_id=1, source_target_pairs={{0,3},{1,0},{2,1},{3,2},{4,7},{5,4},{6,5},{7,6},{8,11},{9,8},{10,9... | collective-permute-start | bytes 122888 | tf_op jit(solution)/shard_map/ppermute | solution.py:617
  28.2 0.9 %copy-start.1 = (f32[208,128]{1,0:T(8,128)S(1)}, f32[208,128]{1,0:T(8,128)}, u32[]{:S(2)}) copy-start(f32[208,128]{1,0:T(8,128)} %get-tuple-element.15.p0) | copy-start | bytes 319492

commit v5 on v4

--- a/solution.py
+++ b/solution.py
@@ -402,12 +402,14 @@
     return jnp.where(block < 8, 2 * block + member, tail)
 
 
-def weights_kernel(
-    p0, p1, p2, p3, tables_ref, win_ref, scale_ref, core_ref, wout_ref, tall
-):
-    col = lax.axis_index("col")
+def own_kernel(p0, scale_ref, own_ref):
     for n in range(4):
         scale_ref[:, n * 128 : (n + 1) * 128] = p0[80 + n * 32 : 112 + n * 32, :]
+    own_ref[...] = p0[:80, :]
+
+
+def weights_kernel(p0, p1, p2, p3, tables_ref, win_ref, core_ref, wout_ref, tall):
+    col = lax.axis_index("col")
     for t, piece in enumerate((p0, p1, p2, p3)):
         source = (col - t + 4) % 4
         high, low = split(piece[:64, :])
@@ -415,7 +417,7 @@
         core_ref[pl.ds(pl.multiple_of(at, 64), 64), :] = high
         core_ref[pl.ds(pl.multiple_of(256 + at, 64), 64), :] = high
         core_ref[pl.ds(pl.multiple_of(512 + at, 64), 64), :] = low
-        tall[pl.ds(pl.multiple_of(source * 16, 16), 16), :] = piece[64:80, :]
+        tall[pl.ds(pl.multiple_of(source * 16, 16), 16), :] = piece[64:, :]
     high, low = split(tall[...])
     spread = dot(jnp.concatenate([high, low], axis=0), table_of(tables_ref, "repeat"))
     zero = jnp.zeros((64, 256), F32)
@@ -576,17 +578,30 @@
     )(got, all_tables()[1], win, scale, core, wout)
 
 
+def own_call(piece):
+    return pl.pallas_call(
+        own_kernel,
+        out_shape=(
+            jax.ShapeDtypeStruct((32, 512), F32),
+            jax.ShapeDtypeStruct((80, 128), F32),
+        ),
+        in_specs=[VMEM],
+        out_specs=(VMEM,) * 2,
+        compiler_params=room(4),
+        name="own_piece",
+    )(piece)
+
+
 def weights_call(pieces):
     return pl.pallas_call(
         weights_kernel,
         out_shape=(
             jax.ShapeDtypeStruct((384, 512), BF16),
-            jax.ShapeDtypeStruct((32, 512), F32),
             jax.ShapeDtypeStruct((768, 128), BF16),
             jax.ShapeDtypeStruct((128, 384), BF16),
         ),
         in_specs=[VMEM] * 5,
-        out_specs=(VMEM,) * 4,
+        out_specs=(VMEM,) * 3,
         scratch_shapes=[pltpu.VMEM((64, 128), F32)],
         compiler_params=room(12),
         name="build_weights",
@@ -611,7 +626,7 @@
 
 def swap_over_col(pieces):
     devices = lax.axis_size("col")
-    arrived = [pieces[0]]
+    arrived = []
     for step in range(1, devices):
         ring = [(n, (n + step) % devices) for n in range(devices)]
         arrived.append(lax.ppermute(pieces[step], "col", ring))
@@ -640,7 +655,8 @@
         out_factor,
     )
     got = everyone(sent)
-    win, scale, core, wout = weights_call(swap_over_col(pieces))
+    scale, own = own_call(pieces[0])
+    win, core, wout = weights_call([own] + swap_over_col(pieces))
     sent = middle_call(got, win, scale, core, wout)
     got = everyone(sent)
     result = inverse_call(got, count, grid_y, grid_z)

time: 63.6 us -> 62.7 us (0.986)
  blocking collectives: 22.8 us -> 21.9 us
    ppermute x3, waiting for transfers between devices: 2.5 us -> 1.59 us  [swap_over_col(): arrived.append(lax.ppermute(pieces[step], 'col', ring))]
    all_to_all x1, blocking collectives: 22.8 us -> 21.9 us  [everyone(): lax.all_to_all(values, ('col', 'gx'), 0, 0, tiled=True).reshape(512, 128)]
    all_to_all x1, waiting for transfers between devices: 7.28 us -> 8.17 us  [everyone(): lax.all_to_all(values, ('col', 'gx'), 0, 0, tiled=True).reshape(512, 128)]
where the time goes in v5:
time: 62.7 us; the launch traced here: 62.6 us
  blocking collectives  21.9 us (35%)
  starting transfers between devices  20.7 us (33%)
  waiting for transfers between devices  9.76 us (16%)
  Pallas kernels  9.34 us (15%)
  local copies, waits for them, and re-layouts  0.9 us (1%)
    all_to_all x1, blocking collectives, everyone(): lax.all_to_all(values, ('col', 'gx'), 0, 0, tiled=True).reshape(512, 128)  21.9 us
    all_to_all x1, starting transfers between devices, everyone(): lax.all_to_all(values, ('col', 'gx'), 0, 0, tiled=True).reshape(512, 128)  15.7 us
    all_to_all x1, waiting for transfers between devices, everyone(): lax.all_to_all(values, ('col', 'gx'), 0, 0, tiled=True).reshape(512, 128)  8.17 us
    ppermute x3, starting transfers between devices, swap_over_col(): arrived.append(lax.ppermute(pieces[step], 'col', ring))  5.01 us
    pallas_call x1, Pallas kernels, forward_call(): pl.pallas_call(forward_kernel, out_shape=(jax.ShapeDtypeStruct((512, 128)...  4.97 us
    pallas_call x1, Pallas kernels, inverse_call(): pl.pallas_call(inverse_kernel, out_shape=jax.ShapeDtypeStruct((count, gri...  2.86 us
    ppermute x3, waiting for transfers between devices, swap_over_col(): arrived.append(lax.ppermute(pieces[step], 'col', ring))  1.59 us
    pallas_call x1, Pallas kernels, middle_call(): pl.pallas_call(middle_kernel, out_shape=jax.ShapeDtypeStruct((512, 128),...  1.3 us
  transfers between devices with their start and end apart: 4, of which 3 were waited for; matrix products, arithmetic and copies ran while one was open for 0% of the time, Pallas kernels for 0%

profile of v5, /device:TPU:1, one launch (start us, length us, event | category | flops | bytes accessed | tf_op | source)
XLA Modules:
  0.0 62.6 jit_solution(15263323366454549436)
XLA Ops:
  0.0 0.0 copy-start
  0.0 5.0 %forward_yz.1 = (f32[512,128]{1,0:T(8,128)}, f32[208,128]{1,0:T(8,128)}, f32[80,128]{1,0:T(8,128)}, f32[80,128]{1,0:T(8,128)}, f32[80,128]{1,0:T(8,128)}) custom-call(bf16[64,256,128]{2,1,0:T(8,128)(2,1)} %bitcast.16, f32[4096,32]{1,0:T(8,128)} %bitcast.17, bf16[80,256]{1,0:T(8,128)(2,1)} %constant.6.clone.ty_ref, bf16[128,256]{1,0:T(8,128)(2,1)} %constant.7.clone.tz_ref, ...), custom_call_target="tpu_custom_call" | custom-call | tf_op jit(solution)/shard_map/forward_yz/pallas_call | solution.py:545
  5.0 15.7 %all-to-all-start = ((f32[256,2,128]{2,1,0:T(2,128)}), f32[256,2,128]{2,1,0:T(2,128)S(1)}, u32[]{:S(2)}, u32[]{:S(2)}) async-start(f32[256,2,128]{2,1,0:T(2,128)} %bitcast.18), calls=%async_computation | async-start | bytes 524288 | tf_op jit(solution)/shard_map/all_to_all | solution.py:638
  20.6 1.4 %collective-permute-start = (f32[80,128]{1,0:T(8,128)}, f32[80,128]{1,0:T(8,128)S(1)}, u32[]{:S(2)}, u32[]{:S(2)}) collective-permute-start(f32[80,128]{1,0:T(8,128)} %get-tuple-element.18), channel_id=1, source_target_pairs={{0,1},{1,2},{2,3},{3,0},{4,5},{5,6},{6,7},{7,4},{8,9},{9,10},{10,1... | collective-permute-start | bytes 122888 | tf_op jit(solution)/shard_map/ppermute | solution.py:632
  22.1 2.5 %collective-permute-start.1 = (f32[80,128]{1,0:T(8,128)}, f32[80,128]{1,0:T(8,128)S(1)}, u32[]{:S(2)}, u32[]{:S(2)}) collective-permute-start(f32[80,128]{1,0:T(8,128)} %get-tuple-element.19), channel_id=1, source_target_pairs={{0,2},{1,3},{2,0},{3,1},{4,6},{5,7},{6,4},{7,5},{8,10},{9,11},{10,... | collective-permute-start | bytes 122888 | tf_op jit(solution)/shard_map/ppermute | solution.py:632
  24.5 1.1 %collective-permute-start.2 = (f32[80,128]{1,0:T(8,128)}, f32[80,128]{1,0:T(8,128)S(1)}, u32[]{:S(2)}, u32[]{:S(2)}) collective-permute-start(f32[80,128]{1,0:T(8,128)} %get-tuple-element.20), channel_id=1, source_target_pairs={{0,3},{1,0},{2,1},{3,2},{4,7},{5,4},{6,5},{7,6},{8,11},{9,8},{10,9... | collective-permute-start | bytes 122888 | tf_op jit(solution)/shard_map/ppermute | solution.py:632
  25.7 0.0 copy-start.1
  25.7 0.9 %copy-done.1 = f32[208,128]{1,0:T(8,128)S(1)} copy-done((f32[208,128]{1,0:T(8,128)S(1)}, f32[208,128]{1,0:T(8,128)}, u32[]{:S(2)}) %copy-start.1) | copy-done | bytes 106520
  26.6 0.0 collective-permute-done.p1
  26.6 0.8 %collective-permute-done.1.p2 = f32[80,128]{1,0:T(8,128)S(1)} collective-permute-done((f32[80,128]{1,0:T(8,128)}, f32[80,128]{1,0:T(8,128)S(1)}, u32[]{:S(2)}, u32[]{:S(2)}) %collective-permute-start.1) | collective-permute-done | bytes 40992 | tf_op jit(solution)/shard_map/ppermute | solution.py:632
  27.4 0.8 %collective-permute-done.2.p3 = f32[80,128]{1,0:T(8,128)S(1)} collective-permute-done((f32[80,128]{1,0:T(8,128)}, f32[80,128]{1,0:T(8,128)S(1)}, u32[]{:S(2)}, u32[]{:S(2)}) %collective-permute-start.2) | collective-permute-done | bytes 40992 | tf_op jit(solution)/shard_map/ppermute | solution.py:632
  28.2 0.0 copy-done
  28.2 0.2 build_weights.1
  28.4 8.2 %all-to-all-done = f32[256,2,128]{2,1,0:T(2,128)S(1)} async-done(((f32[256,2,128]{2,1,0:T(2,128)}), f32[256,2,128]{2,1,0:T(2,128)S(1)}, u32[]{:S(2)}, u32[]{:S(2)}) %all-to-all-start) | async-done | bytes 262176 | tf_op jit(solution)/shard_map/all_to_all | solution.py:638
  36.5 1.3 %mix_columns.1 = f32[512,128]{1,0:T(8,128)S(1)} custom-call(f32[512,128]{1,0:T(8,128)S(1)} %bitcast.13, bf16[4864,128]{1,0:T(8,128)(2,1)S(1)} %copy-done, bf16[384,512]{1,0:T(8,128)(2,1)S(1)} %get-tuple-element.21.win_ref, f32[32,512]{1,0:T(8,128)S(1)} %get-tuple-element.22.scale_ref, bf16[768,128]{1,0:T(8,128)(2,1)S(1)} %get-tuple-element.23.core_ref, ...), custom_call_target="tpu_custom_call" | custom-call | tf_op jit(solution)/shard_map/mix_columns/pallas_call | solution.py:571
  37.9 21.9 %all_to_all.10 = f32[256,2,128]{2,1,0:T(2,128)S(1)} all-to-all(f32[256,2,128]{2,1,0:T(2,128)S(1)} %bitcast.14), channel_id=1, replica_groups=mesh['gx'=64,'col'=4] {'col','gx'}, dimensions={0} | all-to-all | bytes 524288 | tf_op jit(solution)/shard_map/all_to_all | solution.py:638
  59.7 2.9 %inverse_yz.1 = bf16[64,256,128]{2,1,0:T(8,128)(2,1)} custom-call(f32[512,128]{1,0:T(8,128)S(1)} %bitcast.15, bf16[4864,128]{1,0:T(8,128)(2,1)S(1)} %copy-done), custom_call_target="tpu_custom_call" | custom-call | tf_op jit(solution)/shard_map/inverse_yz/pallas_call | solution.py:612
  (1 shorter events, 0.0 us)
Async XLA Ops:
  0.0 28.2 %copy-start = (bf16[4864,128]{1,0:T(8,128)(2,1)S(1)}, bf16[4864,128]{1,0:T(8,128)(2,1)}, u32[]{:S(2)}) copy-start(bf16[4864,128]{1,0:T(8,128)(2,1)} %constant.8.clone.tables_ref) | copy-start | bytes 3735556
  5.0 31.6 %all-to-all-start = ((f32[256,2,128]{2,1,0:T(2,128)}), f32[256,2,128]{2,1,0:T(2,128)S(1)}, u32[]{:S(2)}, u32[]{:S(2)}) async-start(f32[256,2,128]{2,1,0:T(2,128)} %bitcast.18), calls=%async_computation | async-start | bytes 524288 | tf_op jit(solution)/shard_map/all_to_all | solution.py:638
  20.6 5.9 %collective-permute-start = (f32[80,128]{1,0:T(8,128)}, f32[80,128]{1,0:T(8,128)S(1)}, u32[]{:S(2)}, u32[]{:S(2)}) collective-permute-start(f32[80,128]{1,0:T(8,128)} %get-tuple-element.18), channel_id=1, source_target_pairs={{0,1},{1,2},{2,3},{3,0},{4,5},{5,6},{6,7},{7,4},{8,9},{9,10},{10,1... | collective-permute-start | bytes 122888 | tf_op jit(solution)/shard_map/ppermute | solution.py:632
  22.1 5.3 %collective-permute-start.1 = (f32[80,128]{1,0:T(8,128)}, f32[80,128]{1,0:T(8,128)S(1)}, u32[]{:S(2)}, u32[]{:S(2)}) collective-permute-start(f32[80,128]{1,0:T(8,128)} %get-tuple-element.19), channel_id=1, source_target_pairs={{0,2},{1,3},{2,0},{3,1},{4,6},{5,7},{6,4},{7,5},{8,10},{9,11},{10,... | collective-permute-start | bytes 122888 | tf_op jit(solution)/shard_map/ppermute | solution.py:632
  24.5 3.6 %collective-permute-start.2 = (f32[80,128]{1,0:T(8,128)}, f32[80,128]{1,0:T(8,128)S(1)}, u32[]{:S(2)}, u32[]{:S(2)}) collective-permute-start(f32[80,128]{1,0:T(8,128)} %get-tuple-element.20), channel_id=1, source_target_pairs={{0,3},{1,0},{2,1},{3,2},{4,7},{5,4},{6,5},{7,6},{8,11},{9,8},{10,9... | collective-permute-start | bytes 122888 | tf_op jit(solution)/shard_map/ppermute | solution.py:632
  25.7 0.9 %copy-start.1 = (f32[208,128]{1,0:T(8,128)S(1)}, f32[208,128]{1,0:T(8,128)}, u32[]{:S(2)}) copy-start(f32[208,128]{1,0:T(8,128)} %get-tuple-element.16.p0) | copy-start | bytes 319492

commit v6 on v5

--- a/solution.py
+++ b/solution.py
@@ -12,6 +12,7 @@
 
 F32 = jnp.float32
 BF16 = jnp.bfloat16
+ORDER = (0, 2, 1, 3)
 FREQ_ROWS = 18
 ROWS = 40
 PITCH = 68
@@ -283,7 +284,7 @@
     copies[6].wait()
     contract_core(core, high, low, in_rows[...], out_rows[...], sends)
     last = [pltpu.make_async_copy(scale, s0.at[pl.ds(80, 128)], leave.at[0])]
-    for t, target in enumerate((s0.at[pl.ds(0, 80)], s1, s2, s3)):
+    for t, target in zip(ORDER, (s0.at[pl.ds(0, 80)], s1, s2, s3)):
         last.append(pltpu.make_async_copy(sends.at[t], target, leave.at[1 + t]))
     for copy in last:
         copy.start()
@@ -410,7 +411,7 @@
 
 def weights_kernel(p0, p1, p2, p3, tables_ref, win_ref, core_ref, wout_ref, tall):
     col = lax.axis_index("col")
-    for t, piece in enumerate((p0, p1, p2, p3)):
+    for t, piece in zip(ORDER, (p0, p1, p2, p3)):
         source = (col - t + 4) % 4
         high, low = split(piece[:64, :])
         at = source * 64
@@ -627,9 +628,9 @@
 def swap_over_col(pieces):
     devices = lax.axis_size("col")
     arrived = []
-    for step in range(1, devices):
+    for step, piece in zip(ORDER[1:], pieces[1:]):
         ring = [(n, (n + step) % devices) for n in range(devices)]
-        arrived.append(lax.ppermute(pieces[step], "col", ring))
+        arrived.append(lax.ppermute(piece, "col", ring))
     return arrived
 
 

time: 62.7 us -> 63.3 us (level)
    all_to_all x1, waiting for transfers between devices: 8.17 us -> 7.25 us  [everyone(): lax.all_to_all(values, ('col', 'gx'), 0, 0, tiled=True).reshape(512, 128)]
  transfers between devices with their start and end apart: 4 -> 4, of which waited for: 3 -> 2; matrix products, arithmetic and copies ran while one was open for 0% -> 0% of each run, Pallas kernels for 0% -> 0%
where the time goes in v6:
time: 63.3 us; the launch traced here: 63.2 us
  blocking collectives  22.5 us (36%)
  starting transfers between devices  21.3 us (34%)
  Pallas kernels  9.34 us (15%)
  waiting for transfers between devices  9.15 us (14%)
  local copies, waits for them, and re-layouts  0.9 us (1%)
    all_to_all x1, blocking collectives, everyone(): lax.all_to_all(values, ('col', 'gx'), 0, 0, tiled=True).reshape(512, 128)  22.5 us
    all_to_all x1, starting transfers between devices, everyone(): lax.all_to_all(values, ('col', 'gx'), 0, 0, tiled=True).reshape(512, 128)  15.7 us
    all_to_all x1, waiting for transfers between devices, everyone(): lax.all_to_all(values, ('col', 'gx'), 0, 0, tiled=True).reshape(512, 128)  7.25 us
    ppermute x3, starting transfers between devices, swap_over_col(): arrived.append(lax.ppermute(piece, 'col', ring))  5.63 us
    pallas_call x1, Pallas kernels, forward_call(): pl.pallas_call(forward_kernel, out_shape=(jax.ShapeDtypeStruct((512, 128)...  4.97 us
    pallas_call x1, Pallas kernels, inverse_call(): pl.pallas_call(inverse_kernel, out_shape=jax.ShapeDtypeStruct((count, gri...  2.86 us
    ppermute x3, waiting for transfers between devices, swap_over_col(): arrived.append(lax.ppermute(piece, 'col', ring))  1.89 us
    pallas_call x1, Pallas kernels, middle_call(): pl.pallas_call(middle_kernel, out_shape=jax.ShapeDtypeStruct((512, 128),...  1.3 us
  transfers between devices with their start and end apart: 4, of which 2 were waited for; matrix products, arithmetic and copies ran while one was open for 0% of the time, Pallas kernels for 0%

profile of v6, /device:TPU:1, one launch (start us, length us, event | category | flops | bytes accessed | tf_op | source)
XLA Modules:
  0.0 63.2 jit_solution(8739571282117614452)
XLA Ops:
  0.0 0.0 copy-start
  0.0 5.0 %forward_yz.1 = (f32[512,128]{1,0:T(8,128)}, f32[208,128]{1,0:T(8,128)}, f32[80,128]{1,0:T(8,128)}, f32[80,128]{1,0:T(8,128)}, f32[80,128]{1,0:T(8,128)}) custom-call(bf16[64,256,128]{2,1,0:T(8,128)(2,1)} %bitcast.16, f32[4096,32]{1,0:T(8,128)} %bitcast.17, bf16[80,256]{1,0:T(8,128)(2,1)} %constant.6.clone.ty_ref, bf16[128,256]{1,0:T(8,128)(2,1)} %constant.7.clone.tz_ref, ...), custom_call_target="tpu_custom_call" | custom-call | tf_op jit(solution)/shard_map/forward_yz/pallas_call | solution.py:546
  5.0 15.7 %all-to-all-start = ((f32[256,2,128]{2,1,0:T(2,128)}), f32[256,2,128]{2,1,0:T(2,128)S(1)}, u32[]{:S(2)}, u32[]{:S(2)}) async-start(f32[256,2,128]{2,1,0:T(2,128)} %bitcast.18), calls=%async_computation | async-start | bytes 524288 | tf_op jit(solution)/shard_map/all_to_all | solution.py:639
  20.6 3.0 %collective-permute-start = (f32[80,128]{1,0:T(8,128)}, f32[80,128]{1,0:T(8,128)S(1)}, u32[]{:S(2)}, u32[]{:S(2)}) collective-permute-start(f32[80,128]{1,0:T(8,128)} %get-tuple-element.18), channel_id=1, source_target_pairs={{0,2},{1,3},{2,0},{3,1},{4,6},{5,7},{6,4},{7,5},{8,10},{9,11},{10,... | collective-permute-start | bytes 122888 | tf_op jit(solution)/shard_map/ppermute | solution.py:633
  23.6 0.3 collective-permute-start.1
  23.9 2.3 %collective-permute-start.2 = (f32[80,128]{1,0:T(8,128)}, f32[80,128]{1,0:T(8,128)S(1)}, u32[]{:S(2)}, u32[]{:S(2)}) collective-permute-start(f32[80,128]{1,0:T(8,128)} %get-tuple-element.20), channel_id=1, source_target_pairs={{0,3},{1,0},{2,1},{3,2},{4,7},{5,4},{6,5},{7,6},{8,11},{9,8},{10,9... | collective-permute-start | bytes 122888 | tf_op jit(solution)/shard_map/ppermute | solution.py:633
  26.3 0.0 copy-start.1
  26.3 0.9 %copy-done.1 = f32[208,128]{1,0:T(8,128)S(1)} copy-done((f32[208,128]{1,0:T(8,128)S(1)}, f32[208,128]{1,0:T(8,128)}, u32[]{:S(2)}) %copy-start.1) | copy-done | bytes 106520
  27.2 0.0 collective-permute-done.p1
  27.2 1.9 %collective-permute-done.1.p2 = f32[80,128]{1,0:T(8,128)S(1)} collective-permute-done((f32[80,128]{1,0:T(8,128)}, f32[80,128]{1,0:T(8,128)S(1)}, u32[]{:S(2)}, u32[]{:S(2)}) %collective-permute-start.1) | collective-permute-done | bytes 40992 | tf_op jit(solution)/shard_map/ppermute | solution.py:633
  29.1 0.0 collective-permute-done.2.p3
  29.1 0.0 copy-done
  29.1 0.2 build_weights.1
  29.3 7.3 %all-to-all-done = f32[256,2,128]{2,1,0:T(2,128)S(1)} async-done(((f32[256,2,128]{2,1,0:T(2,128)}), f32[256,2,128]{2,1,0:T(2,128)S(1)}, u32[]{:S(2)}, u32[]{:S(2)}) %all-to-all-start) | async-done | bytes 262176 | tf_op jit(solution)/shard_map/all_to_all | solution.py:639
  36.5 1.3 %mix_columns.1 = f32[512,128]{1,0:T(8,128)S(1)} custom-call(f32[512,128]{1,0:T(8,128)S(1)} %bitcast.13, bf16[4864,128]{1,0:T(8,128)(2,1)S(1)} %copy-done, bf16[384,512]{1,0:T(8,128)(2,1)S(1)} %get-tuple-element.21.win_ref, f32[32,512]{1,0:T(8,128)S(1)} %get-tuple-element.22.scale_ref, bf16[768,128]{1,0:T(8,128)(2,1)S(1)} %get-tuple-element.23.core_ref, ...), custom_call_target="tpu_custom_call" | custom-call | tf_op jit(solution)/shard_map/mix_columns/pallas_call | solution.py:572
  37.9 22.5 %all_to_all.10 = f32[256,2,128]{2,1,0:T(2,128)S(1)} all-to-all(f32[256,2,128]{2,1,0:T(2,128)S(1)} %bitcast.14), channel_id=1, replica_groups=mesh['gx'=64,'col'=4] {'col','gx'}, dimensions={0} | all-to-all | bytes 524288 | tf_op jit(solution)/shard_map/all_to_all | solution.py:639
  60.3 2.9 %inverse_yz.1 = bf16[64,256,128]{2,1,0:T(8,128)(2,1)} custom-call(f32[512,128]{1,0:T(8,128)S(1)} %bitcast.15, bf16[4864,128]{1,0:T(8,128)(2,1)S(1)} %copy-done), custom_call_target="tpu_custom_call" | custom-call | tf_op jit(solution)/shard_map/inverse_yz/pallas_call | solution.py:613
  (1 shorter events, 0.0 us)
Async XLA Ops:
  0.0 29.1 %copy-start = (bf16[4864,128]{1,0:T(8,128)(2,1)S(1)}, bf16[4864,128]{1,0:T(8,128)(2,1)}, u32[]{:S(2)}) copy-start(bf16[4864,128]{1,0:T(8,128)(2,1)} %constant.8.clone.tables_ref) | copy-start | bytes 3735556
  5.0 31.6 %all-to-all-start = ((f32[256,2,128]{2,1,0:T(2,128)}), f32[256,2,128]{2,1,0:T(2,128)S(1)}, u32[]{:S(2)}, u32[]{:S(2)}) async-start(f32[256,2,128]{2,1,0:T(2,128)} %bitcast.18), calls=%async_computation | async-start | bytes 524288 | tf_op jit(solution)/shard_map/all_to_all | solution.py:639
  20.6 6.5 %collective-permute-start = (f32[80,128]{1,0:T(8,128)}, f32[80,128]{1,0:T(8,128)S(1)}, u32[]{:S(2)}, u32[]{:S(2)}) collective-permute-start(f32[80,128]{1,0:T(8,128)} %get-tuple-element.18), channel_id=1, source_target_pairs={{0,2},{1,3},{2,0},{3,1},{4,6},{5,7},{6,4},{7,5},{8,10},{9,11},{10,... | collective-permute-start | bytes 122888 | tf_op jit(solution)/shard_map/ppermute | solution.py:633
  23.6 5.5 %collective-permute-start.1 = (f32[80,128]{1,0:T(8,128)}, f32[80,128]{1,0:T(8,128)S(1)}, u32[]{:S(2)}, u32[]{:S(2)}) collective-permute-start(f32[80,128]{1,0:T(8,128)} %get-tuple-element.19), channel_id=1, source_target_pairs={{0,1},{1,2},{2,3},{3,0},{4,5},{5,6},{6,7},{7,4},{8,9},{9,10},{10,1... | collective-permute-start | bytes 122888 | tf_op jit(solution)/shard_map/ppermute | solution.py:633
  23.9 5.1 %collective-permute-start.2 = (f32[80,128]{1,0:T(8,128)}, f32[80,128]{1,0:T(8,128)S(1)}, u32[]{:S(2)}, u32[]{:S(2)}) collective-permute-start(f32[80,128]{1,0:T(8,128)} %get-tuple-element.20), channel_id=1, source_target_pairs={{0,3},{1,0},{2,1},{3,2},{4,7},{5,4},{6,5},{7,6},{8,11},{9,8},{10,9... | collective-permute-start | bytes 122888 | tf_op jit(solution)/shard_map/ppermute | solution.py:633
  26.3 0.9 %copy-start.1 = (f32[208,128]{1,0:T(8,128)S(1)}, f32[208,128]{1,0:T(8,128)}, u32[]{:S(2)}) copy-start(f32[208,128]{1,0:T(8,128)} %get-tuple-element.16.p0) | copy-start | bytes 319492

commit v7 on v6

--- a/solution.py
+++ b/solution.py
@@ -12,7 +12,7 @@
 
 F32 = jnp.float32
 BF16 = jnp.bfloat16
-ORDER = (0, 2, 1, 3)
+ORDER = (0, 1, 3, 2)
 FREQ_ROWS = 18
 ROWS = 40
 PITCH = 68

time: 63.3 us -> 62.4 us (0.986)
  waiting for transfers between devices: 9.15 us -> 10.4 us
  starting transfers between devices: 21.3 us -> 20.1 us
  blocking collectives: 22.5 us -> 21.5 us
    ppermute x3, starting transfers between devices: 5.63 us -> 4.41 us  [swap_over_col(): arrived.append(lax.ppermute(piece, 'col', ring))]
    all_to_all x1, blocking collectives: 22.5 us -> 21.5 us  [everyone(): lax.all_to_all(values, ('col', 'gx'), 0, 0, tiled=True).reshape(512, 128)]
    ppermute x3, waiting for transfers between devices: 1.89 us -> 2.55 us  [swap_over_col(): arrived.append(lax.ppermute(piece, 'col', ring))]
where the time goes in v7:
time: 62.4 us; the launch traced here: 62.3 us
  blocking collectives  21.5 us (34%)
  starting transfers between devices  20.1 us (32%)
  waiting for transfers between devices  10.4 us (17%)
  Pallas kernels  9.34 us (15%)
  local copies, waits for them, and re-layouts  0.9 us (1%)
    all_to_all x1, blocking collectives, everyone(): lax.all_to_all(values, ('col', 'gx'), 0, 0, tiled=True).reshape(512, 128)  21.5 us
    all_to_all x1, starting transfers between devices, everyone(): lax.all_to_all(values, ('col', 'gx'), 0, 0, tiled=True).reshape(512, 128)  15.7 us
    all_to_all x1, waiting for transfers between devices, everyone(): lax.all_to_all(values, ('col', 'gx'), 0, 0, tiled=True).reshape(512, 128)  7.81 us
    pallas_call x1, Pallas kernels, forward_call(): pl.pallas_call(forward_kernel, out_shape=(jax.ShapeDtypeStruct((512, 128)...  4.97 us
    ppermute x3, starting transfers between devices, swap_over_col(): arrived.append(lax.ppermute(piece, 'col', ring))  4.41 us
    pallas_call x1, Pallas kernels, inverse_call(): pl.pallas_call(inverse_kernel, out_shape=jax.ShapeDtypeStruct((count, gri...  2.86 us
    ppermute x3, waiting for transfers between devices, swap_over_col(): arrived.append(lax.ppermute(piece, 'col', ring))  2.55 us
    pallas_call x1, Pallas kernels, middle_call(): pl.pallas_call(middle_kernel, out_shape=jax.ShapeDtypeStruct((512, 128),...  1.3 us
  transfers between devices with their start and end apart: 4, of which 2 were waited for; matrix products, arithmetic and copies ran while one was open for 0% of the time, Pallas kernels for 0%

profile of v7, /device:TPU:1, one launch (start us, length us, event | category | flops | bytes accessed | tf_op | source)
XLA Modules:
  0.0 62.3 jit_solution(6175405849758331007)
XLA Ops:
  0.0 0.0 copy-start
  0.0 5.0 %forward_yz.1 = (f32[512,128]{1,0:T(8,128)}, f32[208,128]{1,0:T(8,128)}, f32[80,128]{1,0:T(8,128)}, f32[80,128]{1,0:T(8,128)}, f32[80,128]{1,0:T(8,128)}) custom-call(bf16[64,256,128]{2,1,0:T(8,128)(2,1)} %bitcast.16, f32[4096,32]{1,0:T(8,128)} %bitcast.17, bf16[80,256]{1,0:T(8,128)(2,1)} %constant.6.clone.ty_ref, bf16[128,256]{1,0:T(8,128)(2,1)} %constant.7.clone.tz_ref, ...), custom_call_target="tpu_custom_call" | custom-call | tf_op jit(solution)/shard_map/forward_yz/pallas_call | solution.py:546
  5.0 15.7 %all-to-all-start = ((f32[256,2,128]{2,1,0:T(2,128)}), f32[256,2,128]{2,1,0:T(2,128)S(1)}, u32[]{:S(2)}, u32[]{:S(2)}) async-start(f32[256,2,128]{2,1,0:T(2,128)} %bitcast.18), calls=%async_computation | async-start | bytes 524288 | tf_op jit(solution)/shard_map/all_to_all | solution.py:639
  20.6 1.4 %collective-permute-start = (f32[80,128]{1,0:T(8,128)}, f32[80,128]{1,0:T(8,128)S(1)}, u32[]{:S(2)}, u32[]{:S(2)}) collective-permute-start(f32[80,128]{1,0:T(8,128)} %get-tuple-element.18), channel_id=1, source_target_pairs={{0,1},{1,2},{2,3},{3,0},{4,5},{5,6},{6,7},{7,4},{8,9},{9,10},{10,1... | collective-permute-start | bytes 122888 | tf_op jit(solution)/shard_map/ppermute | solution.py:633
  22.1 1.4 %collective-permute-start.1 = (f32[80,128]{1,0:T(8,128)}, f32[80,128]{1,0:T(8,128)S(1)}, u32[]{:S(2)}, u32[]{:S(2)}) collective-permute-start(f32[80,128]{1,0:T(8,128)} %get-tuple-element.19), channel_id=1, source_target_pairs={{0,3},{1,0},{2,1},{3,2},{4,7},{5,4},{6,5},{7,6},{8,11},{9,8},{10,9... | collective-permute-start | bytes 122888 | tf_op jit(solution)/shard_map/ppermute | solution.py:633
  23.4 1.6 %collective-permute-start.2 = (f32[80,128]{1,0:T(8,128)}, f32[80,128]{1,0:T(8,128)S(1)}, u32[]{:S(2)}, u32[]{:S(2)}) collective-permute-start(f32[80,128]{1,0:T(8,128)} %get-tuple-element.20), channel_id=1, source_target_pairs={{0,2},{1,3},{2,0},{3,1},{4,6},{5,7},{6,4},{7,5},{8,10},{9,11},{10,... | collective-permute-start | bytes 122888 | tf_op jit(solution)/shard_map/ppermute | solution.py:633
  25.1 0.0 copy-start.1
  25.1 0.9 %copy-done.1 = f32[208,128]{1,0:T(8,128)S(1)} copy-done((f32[208,128]{1,0:T(8,128)S(1)}, f32[208,128]{1,0:T(8,128)}, u32[]{:S(2)}) %copy-start.1) | copy-done | bytes 106520
  26.0 0.0 collective-permute-done.p1
  26.0 0.0 collective-permute-done.1.p2
  26.0 2.5 %collective-permute-done.2.p3 = f32[80,128]{1,0:T(8,128)S(1)} collective-permute-done((f32[80,128]{1,0:T(8,128)}, f32[80,128]{1,0:T(8,128)S(1)}, u32[]{:S(2)}, u32[]{:S(2)}) %collective-permute-start.2) | collective-permute-done | bytes 40992 | tf_op jit(solution)/shard_map/ppermute | solution.py:633
  28.5 0.0 copy-done
  28.5 0.2 build_weights.1
  28.7 7.8 %all-to-all-done = f32[256,2,128]{2,1,0:T(2,128)S(1)} async-done(((f32[256,2,128]{2,1,0:T(2,128)}), f32[256,2,128]{2,1,0:T(2,128)S(1)}, u32[]{:S(2)}, u32[]{:S(2)}) %all-to-all-start) | async-done | bytes 262176 | tf_op jit(solution)/shard_map/all_to_all | solution.py:639
  36.5 1.3 %mix_columns.1 = f32[512,128]{1,0:T(8,128)S(1)} custom-call(f32[512,128]{1,0:T(8,128)S(1)} %bitcast.13, bf16[4864,128]{1,0:T(8,128)(2,1)S(1)} %copy-done, bf16[384,512]{1,0:T(8,128)(2,1)S(1)} %get-tuple-element.21.win_ref, f32[32,512]{1,0:T(8,128)S(1)} %get-tuple-element.22.scale_ref, bf16[768,128]{1,0:T(8,128)(2,1)S(1)} %get-tuple-element.23.core_ref, ...), custom_call_target="tpu_custom_call" | custom-call | tf_op jit(solution)/shard_map/mix_columns/pallas_call | solution.py:572
  37.9 21.5 %all_to_all.10 = f32[256,2,128]{2,1,0:T(2,128)S(1)} all-to-all(f32[256,2,128]{2,1,0:T(2,128)S(1)} %bitcast.14), channel_id=1, replica_groups=mesh['gx'=64,'col'=4] {'col','gx'}, dimensions={0} | all-to-all | bytes 524288 | tf_op jit(solution)/shard_map/all_to_all | solution.py:639
  59.4 2.9 %inverse_yz.1 = bf16[64,256,128]{2,1,0:T(8,128)(2,1)} custom-call(f32[512,128]{1,0:T(8,128)S(1)} %bitcast.15, bf16[4864,128]{1,0:T(8,128)(2,1)S(1)} %copy-done), custom_call_target="tpu_custom_call" | custom-call | tf_op jit(solution)/shard_map/inverse_yz/pallas_call | solution.py:613
  (1 shorter events, 0.0 us)
Async XLA Ops:
  0.0 28.5 %copy-start = (bf16[4864,128]{1,0:T(8,128)(2,1)S(1)}, bf16[4864,128]{1,0:T(8,128)(2,1)}, u32[]{:S(2)}) copy-start(bf16[4864,128]{1,0:T(8,128)(2,1)} %constant.8.clone.tables_ref) | copy-start | bytes 3735556
  5.0 31.6 %all-to-all-start = ((f32[256,2,128]{2,1,0:T(2,128)}), f32[256,2,128]{2,1,0:T(2,128)S(1)}, u32[]{:S(2)}, u32[]{:S(2)}) async-start(f32[256,2,128]{2,1,0:T(2,128)} %bitcast.18), calls=%async_computation | async-start | bytes 524288 | tf_op jit(solution)/shard_map/all_to_all | solution.py:639
  20.6 5.3 %collective-permute-start = (f32[80,128]{1,0:T(8,128)}, f32[80,128]{1,0:T(8,128)S(1)}, u32[]{:S(2)}, u32[]{:S(2)}) collective-permute-start(f32[80,128]{1,0:T(8,128)} %get-tuple-element.18), channel_id=1, source_target_pairs={{0,1},{1,2},{2,3},{3,0},{4,5},{5,6},{6,7},{7,4},{8,9},{9,10},{10,1... | collective-permute-start | bytes 122888 | tf_op jit(solution)/shard_map/ppermute | solution.py:633
  22.1 3.9 %collective-permute-start.1 = (f32[80,128]{1,0:T(8,128)}, f32[80,128]{1,0:T(8,128)S(1)}, u32[]{:S(2)}, u32[]{:S(2)}) collective-permute-start(f32[80,128]{1,0:T(8,128)} %get-tuple-element.19), channel_id=1, source_target_pairs={{0,3},{1,0},{2,1},{3,2},{4,7},{5,4},{6,5},{7,6},{8,11},{9,8},{10,9... | collective-permute-start | bytes 122888 | tf_op jit(solution)/shard_map/ppermute | solution.py:633
  23.4 5.1 %collective-permute-start.2 = (f32[80,128]{1,0:T(8,128)}, f32[80,128]{1,0:T(8,128)S(1)}, u32[]{:S(2)}, u32[]{:S(2)}) collective-permute-start(f32[80,128]{1,0:T(8,128)} %get-tuple-element.20), channel_id=1, source_target_pairs={{0,2},{1,3},{2,0},{3,1},{4,6},{5,7},{6,4},{7,5},{8,10},{9,11},{10,... | collective-permute-start | bytes 122888 | tf_op jit(solution)/shard_map/ppermute | solution.py:633
  25.1 0.9 %copy-start.1 = (f32[208,128]{1,0:T(8,128)S(1)}, f32[208,128]{1,0:T(8,128)}, u32[]{:S(2)}) copy-start(f32[208,128]{1,0:T(8,128)} %get-tuple-element.16.p0) | copy-start | bytes 319492
